TPU v7x, 32 devices: a whole 2x2x4 slice. The times are simulated.
32 devices in a mesh: span: 8 (over y, x, core), head: 4 (over z).
Axes of the slice: x: 2, y: 2, z: 4, core: 2. Of those that a mesh axis runs over, the one named last changes fastest.
Arguments:
- decoder_states: bfloat16 [16384, 1024], P('span'), may hold values from -21 to 21
- encodings: bfloat16 [512, 128, 1024], P('span', 'head'), may hold values from -21 to 21
- neighbor_table: int32 [256, 2, 2], P('span'), may hold values from 0 to 63, as said below
- query_weight: bfloat16 [1024, 1024], P(None, 'head'), may hold values from -0.1875 to 0.1875
- key_weight: bfloat16 [1024, 1024], P(None, 'head'), may hold values from -0.1875 to 0.1875
- value_weight: bfloat16 [1024, 1024], P(None, 'head'), may hold values from -0.1875 to 0.1875
- out_weight: bfloat16 [1024, 1024], P('head'), may hold values from -0.1875 to 0.1875
Outputs:
- attended: bfloat16 [16384, 1024], P('span', 'head')
Inputs may be any that keep to these rules, and one draw needn't show every extreme that they name: neighbor_table[c, k, 0] is the database shard and neighbor_table[c, k, 1] the slot in that shard of neighbor k of span c; in each aligned block of 32 spans (the spans of one device along `span`) every shard is named by exactly one neighbor, and every slot of every shard is named exactly once in the whole table.
All inputs are finite; a program needn't handle non-finite values.
Results may differ from a plain program's by a relative error of at most 0.012.
The roundings to bfloat16 on the way count: a program that leaves them out, or rounds other values in their place, can miss the bound.
Values may be sent and summed in bfloat16 or wider, within the bound.
A program may use at most 128 MiB of HBM per device.

v0:
```python
import functools

import jax
import jax.numpy as jnp
from jax import lax
from jax.experimental import pallas as pl
from jax.experimental.pallas import tpu as pltpu
from jax.sharding import PartitionSpec as P

HEAD_DIM = 64
SPAN_LEN = 64
SEQ_LEN = 2048
VMEM = 56 * 1024 * 1024
CHUNKS = 2


def matmul_kernel(x_ref, w_ref, o_ref):
    groups = w_ref.shape[1]
    cols = w_ref.shape[3]
    x = x_ref[...]
    for g in range(groups):
        w = w_ref[:, g].reshape(x_ref.shape[1], cols)
        o_ref[:, g * cols : (g + 1) * cols] = jnp.dot(
            x, w, preferred_element_type=jnp.float32
        ).astype(o_ref.dtype)


def grouped_matmul(x, w, cols, col_block, tile):
    peers, groups, depth, _ = w.shape
    rows, width = x.shape
    return pl.pallas_call(
        matmul_kernel,
        out_shape=jax.ShapeDtypeStruct((rows, groups * cols), jnp.bfloat16),
        grid=(rows // tile,),
        in_specs=[
            pl.BlockSpec((tile, width), lambda i: (i, 0)),
            pl.BlockSpec((peers, groups, depth, cols), lambda i: (0, 0, 0, col_block)),
        ],
        out_specs=pl.BlockSpec((tile, groups * cols), lambda i: (i, 0)),
        compiler_params=pltpu.CompilerParams(vmem_limit_bytes=VMEM),
        cost_estimate=pl.CostEstimate(
            flops=2 * rows * width * groups * cols, bytes_accessed=16 << 20, transcendentals=0
        ),
    )(x, w)


def attend_kernel(position_ref, *refs, spans, neighbors, group_cols):
    kv_refs = refs[: spans * neighbors]
    q_ref, ctx_ref, lse_ref, top_ref, s_ref, e_ref = refs[spans * neighbors :]
    width = q_ref.shape[1]
    heads = width // HEAD_DIM
    groups = width // group_cols
    packed = group_cols // HEAD_DIM
    tokens = kv_refs[0].shape[1]
    keys = neighbors * tokens
    wide = packed * keys
    row_head = lax.broadcasted_iota(jnp.int32, (wide, group_cols), 0) // keys
    col_head = lax.broadcasted_iota(jnp.int32, (wide, group_cols), 1) // HEAD_DIM
    diagonal = row_head == col_head
    pair = 128 // keys
    lane_head = lax.broadcasted_iota(jnp.int32, (SPAN_LEN, 128), 1) // keys
    lane = lax.broadcasted_iota(jnp.int32, (SPAN_LEN, 128), 1)
    collect = (
        lax.broadcasted_iota(jnp.int32, (heads * keys, 128), 0) // keys
        == lax.broadcasted_iota(jnp.int32, (heads * keys, 128), 1)
    ).astype(jnp.bfloat16)

    def widened(c, base):
        part = jnp.concatenate(
            [kv_refs[c * neighbors + k][0, :, base : base + group_cols] for k in range(neighbors)],
            axis=0,
        )
        return jnp.where(diagonal, jnp.concatenate([part] * packed, axis=0), 0)

    for c in range(spans):
        row = slice(c * SPAN_LEN, (c + 1) * SPAN_LEN)
        for g in range(groups):
            s_ref[row, g * wide : (g + 1) * wide] = lax.dot_general(
                q_ref[row, g * group_cols : (g + 1) * group_cols],
                widened(c, g * 2 * group_cols),
                (((1,), (1,)), ((), ())),
                preferred_element_type=jnp.float32,
            ) * (HEAD_DIM ** (-0.5))
    tops = []
    for c in range(spans):
        row = slice(c * SPAN_LEN, (c + 1) * SPAN_LEN)
        top_all = jnp.zeros((SPAN_LEN, 128), jnp.float32)
        for t in range(heads // pair):
            s = s_ref[row, t * 128 : (t + 1) * 128]
            top = None
            for n in range(pair):
                m = jnp.max(
                    jnp.where(lane_head == n, s, -jnp.inf), axis=1, keepdims=True
                )
                top = m if top is None else jnp.where(lane_head == n, m, top)
                top_all = jnp.where(lane == t * pair + n, m, top_all)
            e_ref[row, t * 128 : (t + 1) * 128] = jnp.exp(s - top).astype(jnp.bfloat16)
        tops.append(top_all)
    top_all = jnp.concatenate(tops, axis=0)
    total = jnp.dot(e_ref[...], collect, preferred_element_type=jnp.float32)
    top_rows = top_all.T[:heads]
    top_ref[...] = top_rows
    lse_ref[...] = top_rows + jnp.log(total.T[:heads])
    for c in range(spans):
        row = slice(c * SPAN_LEN, (c + 1) * SPAN_LEN)
        for g in range(groups):
            ctx_ref[row, g * group_cols : (g + 1) * group_cols] = jnp.dot(
                e_ref[row, g * wide : (g + 1) * wide],
                widened(c, g * 2 * group_cols + group_cols),
                preferred_element_type=jnp.float32,
            ).astype(ctx_ref.dtype)


def attend(position, q, kv, first, span_count, neighbors, group_cols, spans=4):
    width = q.shape[1]
    rows = span_count * SPAN_LEN
    heads = width // HEAD_DIM
    _, tokens, wide = kv.shape
    score_cols = heads * neighbors * tokens
    begin = first // spans
    step_rows = spans * SPAN_LEN

    def neighbor_spec(j):
        return pl.BlockSpec(
            (1, tokens, wide),
            lambda i, p: (p[(i + begin) * (spans * neighbors) + j], 0, 0),
        )

    return pl.pallas_call(
        functools.partial(
            attend_kernel, spans=spans, neighbors=neighbors, group_cols=group_cols
        ),
        out_shape=(
            jax.ShapeDtypeStruct((rows, width), jnp.bfloat16),
            jax.ShapeDtypeStruct((heads, rows), jnp.float32),
            jax.ShapeDtypeStruct((heads, rows), jnp.float32),
        ),
        grid_spec=pltpu.PrefetchScalarGridSpec(
            num_scalar_prefetch=1,
            grid=(span_count // spans,),
            in_specs=[neighbor_spec(j) for j in range(spans * neighbors)]
            + [pl.BlockSpec((step_rows, width), lambda i, p: (i + begin, 0))],
            out_specs=[
                pl.BlockSpec((step_rows, width), lambda i, p: (i, 0)),
                pl.BlockSpec((heads, step_rows), lambda i, p: (0, i)),
                pl.BlockSpec((heads, step_rows), lambda i, p: (0, i)),
            ],
            scratch_shapes=[
                pltpu.VMEM((step_rows, score_cols), jnp.float32),
                pltpu.VMEM((step_rows, score_cols), jnp.bfloat16),
            ],
        ),
        compiler_params=pltpu.CompilerParams(vmem_limit_bytes=VMEM),
        cost_estimate=pl.CostEstimate(
            flops=span_count << 28, bytes_accessed=16 << 20, transcendentals=span_count << 16
        ),
    )(position, *([kv] * (spans * neighbors)), q)


def project_kernel(ctx_ref, own_ref, all_ref, w_ref, o_ref):
    every = all_ref[...]
    top = jnp.max(every, axis=0)
    total = jnp.sum(jnp.exp(every - top[None]), axis=0)
    scale = jnp.exp(own_ref[...] - top) / total
    high = scale.astype(jnp.bfloat16)
    low = (scale - high.astype(jnp.float32)).astype(jnp.bfloat16)
    heads = scale.shape[0]
    width = ctx_ref.shape[1]
    spread = (
        lax.broadcasted_iota(jnp.int32, (2 * heads, width), 0) % heads
        == lax.broadcasted_iota(jnp.int32, (2 * heads, width), 1) // HEAD_DIM
    ).astype(jnp.bfloat16)
    factor = lax.dot_general(
        jnp.concatenate([high, low], axis=0),
        spread,
        (((0,), (0,)), ((), ())),
        preferred_element_type=jnp.float32,
    )
    scaled = (ctx_ref[...].astype(jnp.float32) * factor).astype(jnp.bfloat16)
    o_ref[...] = jnp.dot(scaled, w_ref[...], preferred_element_type=jnp.float32).astype(
        o_ref.dtype
    )


def project(ctx, own, every, w, tile=256):
    rows, width = ctx.shape
    groups, heads, _ = every.shape
    return pl.pallas_call(
        project_kernel,
        out_shape=jax.ShapeDtypeStruct((rows, w.shape[1]), jnp.bfloat16),
        grid=(rows // tile,),
        in_specs=[
            pl.BlockSpec((tile, width), lambda i: (i, 0)),
            pl.BlockSpec((heads, tile), lambda i: (0, i)),
            pl.BlockSpec((groups, heads, tile), lambda i: (0, 0, i)),
            pl.BlockSpec(w.shape, lambda i: (0, 0)),
        ],
        out_specs=pl.BlockSpec((tile, w.shape[1]), lambda i: (i, 0)),
        compiler_params=pltpu.CompilerParams(vmem_limit_bytes=VMEM),
        cost_estimate=pl.CostEstimate(
            flops=2 * rows * width * w.shape[1], bytes_accessed=6 << 20, transcendentals=0
        ),
    )(ctx, own, every, w)


def body(
    decoder_states, encodings, neighbor_table, query_weight, key_weight, value_weight, out_weight
):
    peer_count = lax.axis_size("span")
    groups = lax.axis_size("head")
    model_width = decoder_states.shape[1]
    group_cols = query_weight.shape[1]
    me = lax.axis_index("span")
    packed = jnp.concatenate([key_weight, value_weight, query_weight], axis=1)
    part = model_width // peer_count
    packed = lax.dynamic_slice_in_dim(packed, me * part, part, 0)
    gathered = lax.all_gather(packed, ("span", "head"), axis=0, tiled=False)
    gathered = gathered.reshape(peer_count, groups, part, 3 * group_cols)
    shard_ids = neighbor_table[:, :, 0].reshape(-1)
    slot_ids = neighbor_table[:, :, 1].reshape(-1)
    entries = shard_ids.shape[0]
    per_peer = entries // peer_count
    numbering = jnp.arange(entries, dtype=jnp.int32)
    same_before = (shard_ids[:, None] == shard_ids[None, :]) & (
        numbering[None, :] < numbering[:, None]
    )
    ranking = jnp.sum(same_before.astype(jnp.int32), axis=1)
    position = shard_ids * per_peer + ranking
    placed = position[None, :] == numbering[:, None]
    request = jnp.sum(jnp.where(placed, slot_ids[None, :], 0), axis=1)
    wanted = lax.all_to_all(request, "span", split_axis=0, concat_axis=0, tiled=True)
    wanted, late_out = lax.optimization_barrier((wanted, out_weight))
    out_all = lax.all_gather(late_out, "head", axis=0, tiled=True)
    selected = encodings[wanted]
    arrived = lax.all_to_all(selected, "span", split_axis=0, concat_axis=0, tiled=True)

    sequences = decoder_states.shape[0] // SEQ_LEN
    offset = SPAN_LEN - 1
    states = decoder_states.reshape(sequences, SEQ_LEN, model_width)
    states = jnp.concatenate(
        [states[:, offset:], jnp.zeros((sequences, offset, model_width), states.dtype)], axis=1
    ).reshape(-1, model_width)
    tile = 512
    queries = grouped_matmul(states, gathered, group_cols, 2, tile)
    kv = grouped_matmul(arrived.reshape(-1, model_width), gathered, 2 * group_cols, 0, tile)
    kv = kv.reshape(entries, arrived.shape[1], -1)
    span_count, neighbors = neighbor_table.shape[:2]
    pieces = []
    chunk = span_count // CHUNKS
    for first in range(0, span_count, chunk):
        context, lse, top = attend(position, queries, kv, first, chunk, neighbors, group_cols)
        every = lax.all_gather(lse, "head", axis=0, tiled=False)
        partial = project(context, top, every, out_all)
        pieces.append(lax.psum_scatter(partial, "head", scatter_dimension=1, tiled=True))
    summed = jnp.concatenate(pieces, axis=0)
    summed = summed.reshape(sequences, SEQ_LEN, -1)
    summed = jnp.concatenate(
        [jnp.zeros((sequences, offset, summed.shape[2]), summed.dtype), summed[:, :-offset]], axis=1
    )
    return summed.reshape(decoder_states.shape[0], -1)


def solution(mesh):
    return jax.shard_map(
        body,
        mesh=mesh,
        in_specs=(
            P("span", None),
            P("span", "head", None),
            P("span", None, None),
            P(None, "head"),
            P(None, "head"),
            P(None, "head"),
            P("head", None),
        ),
        out_specs=P("span", "head"),
        check_vma=False,
    )
```

profile of v0, /device:TPU:0, one launch (start us, length us, event | category | flops | bytes accessed | tf_op | source)
XLA Modules:
  0.0 261.0 jit_solution(10480377056315314342)
XLA Ops:
  6.5 0.0 all-gather.8.cloned.1.call-start
  6.5 1.6 fusion.1
  8.1 0.0 all-gather.8.cloned.1.call-update
  8.2 0.8 fusion.3
  8.9 0.1 copy.15
  9.0 0.1 reshape_squeeze.3
  9.1 0.1 copy.16
  9.2 0.1 broadcast_in_dim.23
  9.3 0.2 convert_reduce_fusion
  9.5 0.0 copy-start
  9.5 0.1 select_reduce_fusion
  9.6 0.1 all_to_all.11
  9.7 9.7 %all_to_all.17 = s32[8,8,1]{1,2,0:T(1,128)S(1)} all-to-all(s32[8,8,1]{1,2,0:T(1,128)S(1)} %bitcast.37), channel_id=1, replica_groups=mesh['span'=8,'head'=4] {'span'}, dimensions={0} | all-to-all | bytes 512 | tf_op jit(solution)/shard_map/all_to_all | solution.py:231
  19.4 0.5 broadcast.15
  19.9 0.6 reduce.3
  20.6 0.1 all_to_all.13
  20.7 5.1 %gather_fusion = bf16[64,32,1024]{2,1,0:T(8,128)(2,1)} fusion(bf16[64,32,1024]{2,1,0:T(8,128)(2,1)} %param.8, s32[1024]{0:T(1024)S(1)} %pad_clamp_fusion), kind=kCustom, calls=%fused_computation | custom fusion | bytes 8388864 | tf_op jit(solution)/shard_map/gather | solution.py:234
  25.7 0.0 copy-done
  25.7 4.6 %all-to-all-start.1 = ((bf16[64,32,1024]{2,1,0:T(8,128)(2,1)}), bf16[64,32,1024]{2,1,0:T(8,128)(2,1)}, u32[]{:S(2)}, u32[]{:S(2)}) async-start(bf16[64,32,1024]{2,1,0:T(8,128)(2,1)} %gather_fusion), calls=%async_computation.1 | async-start | bytes 8388608 | tf_op jit(solution)/shard_map/all_to_all | solution.py:235
  30.3 0.0 all-gather.6.cloned.1.call-start
  30.3 0.7 all-gather.6.cloned.1.call-update
  31.0 0.0 reduce-scatter.3.cloned.1.call-start
  31.1 3.3 %slice.18 = bf16[1,1985,1024]{2,1,0:T(8,128)(2,1)S(1)} slice(bf16[1,2048,1024]{2,1,0:T(8,128)(2,1)} %bitcast.34), slice={[0:1], [63:2048], [0:1024]} | slice | bytes 8130560 | tf_op jit(solution)/shard_map/slice | solution.py:241
  34.3 2.4 pad_bitcast_fusion.x_ref
  36.7 62.2 %all-gather.8.cloned.1.call-done = bf16[4096,768]{1,0:T(8,128)(2,1)} async-done(((bf16[128,768]{1,0:T(8,128)(2,1)}), bf16[4096,768]{1,0:T(8,128)(2,1)}) %all-gather.8.cloned.1.call-update) | async-done | bytes 6291472 | tf_op jit(solution)/shard_map/all_gather | solution.py:217
  98.9 8.4 %shard_map.74.refs_8_ = bf16[2048,1024]{1,0:T(8,128)(2,1)} custom-call(bf16[2048,1024]{1,0:T(8,128)(2,1)} %pad_bitcast_fusion.x_ref, bf16[8,4,128,768]{3,2,1,0:T(8,128)(2,1)} %bitcast.38), custom_call_target="tpu_custom_call" | custom-call | flops 4294967296 | bytes 16777216 | tf_op jit(solution)/shard_map/pallas_call | solution.py:31
  107.3 0.0 all-to-all-done.1
  107.3 13.3 %shard_map.73 = bf16[2048,2048]{1,0:T(8,128)(2,1)} custom-call(bf16[2048,1024]{1,0:T(8,128)(2,1)} %bitcast.1.x_ref, bf16[8,4,128,768]{3,2,1,0:T(8,128)(2,1)} %bitcast.39), custom_call_target="tpu_custom_call" | custom-call | flops 8589934592 | bytes 16777216 | tf_op jit(solution)/shard_map/pallas_call | solution.py:31
  120.6 9.4 %shard_map.75 = (bf16[1024,1024]{1,0:T(8,128)(2,1)}, f32[16,1024]{1,0:T(8,128)}, f32[16,1024]{1,0:T(8,128)}) custom-call(s32[64]{0:T(128)} %copy-done, bf16[64,32,2048]{2,1,0:T(8,128)(2,1)} %bitcast.18, bf16[64,32,2048]{2,1,0:T(8,128)(2,1)} %bitcast.19, bf16[64,32,2048]{2,1,0:T(8,128)(2,1)} %bitcast.20, bf16[64,32,2048]{2,1,0:T(8,128)(2,1)} %bitcast.21, ...), custom_call_target="tpu_custom_call" | custom-call | flops 4294967296 | bytes 16777216 | tf_op jit(solution)/shard_map/pallas_call | solution.py:129
  129.9 17.3 %all-gather.1 = f32[64,1024]{1,0:T(8,128)} all-gather(f32[16,1024]{1,0:T(8,128)} %get-tuple-element.16), channel_id=3, replica_groups=mesh['span'=8,'head'=4] {'head'}, dimensions={0}, use_global_device_ids=true | all-gather | bytes 327680 | tf_op jit(solution)/shard_map/all_gather | solution.py:252
  147.3 6.2 %all-gather.6.cloned.1.call-done.w_ref = bf16[1024,1024]{1,0:T(8,128)(2,1)} async-done(((bf16[256,1024]{1,0:T(8,128)(2,1)}), bf16[1024,1024]{1,0:T(8,128)(2,1)}) %all-gather.6.cloned.1.call-update) | async-done | bytes 2097168 | tf_op jit(solution)/shard_map/all_gather | solution.py:233
  153.5 6.6 %shard_map.76 = bf16[1024,1024]{1,0:T(8,128)(2,1)} custom-call(bf16[1024,1024]{1,0:T(8,128)(2,1)} %get-tuple-element.14.ctx_ref, f32[16,1024]{1,0:T(8,128)} %get-tuple-element.15.own_ref, f32[4,16,1024]{2,1,0:T(8,128)} %bitcast.35, bf16[1024,1024]{1,0:T(8,128)(2,1)} %all-gather.6.cloned.1.call-done.w_ref), custom_call_target="tpu_custom_call" | custom-call | flops 2147483648 | bytes 6291456 | tf_op jit(solution)/shard_map/pallas_call | solution.py:188
  160.1 0.0 reduce-scatter.3.cloned.1.call-update
  160.1 0.0 reduce-scatter.5.cloned.1.call-start
  160.1 9.6 %shard_map.77 = (bf16[1024,1024]{1,0:T(8,128)(2,1)}, f32[16,1024]{1,0:T(8,128)}, f32[16,1024]{1,0:T(8,128)}) custom-call(s32[64]{0:T(128)} %copy-done, bf16[64,32,2048]{2,1,0:T(8,128)(2,1)} %bitcast.26, bf16[64,32,2048]{2,1,0:T(8,128)(2,1)} %bitcast.27, bf16[64,32,2048]{2,1,0:T(8,128)(2,1)} %bitcast.28, bf16[64,32,2048]{2,1,0:T(8,128)(2,1)} %bitcast.29, ...), custom_call_target="tpu_custom_call" | custom-call | flops 4294967296 | bytes 16777216 | tf_op jit(solution)/shard_map/pallas_call | solution.py:129
  169.7 17.3 %all-gather.2 = f32[64,1024]{1,0:T(8,128)} all-gather(f32[16,1024]{1,0:T(8,128)} %get-tuple-element.20), channel_id=4, replica_groups=mesh['span'=8,'head'=4] {'head'}, dimensions={0}, use_global_device_ids=true | all-gather | bytes 327680 | tf_op jit(solution)/shard_map/all_gather | solution.py:252
  187.1 6.6 %shard_map.78 = bf16[1024,1024]{1,0:T(8,128)(2,1)} custom-call(bf16[1024,1024]{1,0:T(8,128)(2,1)} %get-tuple-element.18.ctx_ref, f32[16,1024]{1,0:T(8,128)} %get-tuple-element.19.own_ref, f32[4,16,1024]{2,1,0:T(8,128)} %bitcast.36, bf16[1024,1024]{1,0:T(8,128)(2,1)} %all-gather.6.cloned.1.call-done.w_ref), custom_call_target="tpu_custom_call" | custom-call | flops 2147483648 | bytes 6291456 | tf_op jit(solution)/shard_map/pallas_call | solution.py:188
  193.7 0.0 reduce-scatter.5.cloned.1.call-update
  193.7 13.2 %reduce-scatter.3.cloned.1.call-done = bf16[1024,256]{1,0:T(8,128)(2,1)} async-done(((bf16[1024,1024]{1,0:T(8,128)(2,1)}), bf16[1024,256]{1,0:T(8,128)(2,1)}) %reduce-scatter.3.cloned.1.call-update) | async-done | bytes 524304 | tf_op jit(solution)/shard_map/reduce_scatter | solution.py:254
  206.9 45.0 %reduce-scatter.5.cloned.1.call-done = bf16[1024,256]{1,0:T(8,128)(2,1)} async-done(((bf16[1024,1024]{1,0:T(8,128)(2,1)}), bf16[1024,256]{1,0:T(8,128)(2,1)}) %reduce-scatter.5.cloned.1.call-update) | async-done | bytes 524304 | tf_op jit(solution)/shard_map/reduce_scatter | solution.py:254
  251.9 1.3 maximum_bitcast_fusion
  253.2 0.1 slice.19
  253.3 1.2 pad_bitcast_fusion.1
  (3 shorter events, 0.0 us)
Async XLA Ops:
  6.5 92.4 %all-gather.8.cloned.1.call-start = ((), (), s32[]{:S(2)}) async-start(), calls=%async_computation.7 | async-start | bytes 6488064 | tf_op jit(solution)/shard_map/all_gather | solution.py:217
  9.5 16.2 %copy-start = (s32[64]{0:T(128)}, s32[64]{0:T(128)S(1)}, u32[]{:S(2)}) copy-start(s32[64]{0:T(128)S(1)} %multiply_add_fusion.position_ref) | copy-start | bytes 772
  25.7 81.6 %all-to-all-start.1 = ((bf16[64,32,1024]{2,1,0:T(8,128)(2,1)}), bf16[64,32,1024]{2,1,0:T(8,128)(2,1)}, u32[]{:S(2)}, u32[]{:S(2)}) async-start(bf16[64,32,1024]{2,1,0:T(8,128)(2,1)} %gather_fusion), calls=%async_computation.1 | async-start | bytes 8388608 | tf_op jit(solution)/shard_map/all_to_all | solution.py:235
  30.3 123.2 %all-gather.6.cloned.1.call-start = ((), (), s32[]{:S(2)}) async-start(), calls=%async_computation.4 | async-start | bytes 2621440 | tf_op jit(solution)/shard_map/all_gather | solution.py:233
  31.0 175.9 %reduce-scatter.3.cloned.1.call-start = ((), (), s32[]{:S(2)}) async-start(), calls=%async_computation.5 | async-start | bytes 2621440 | tf_op jit(solution)/shard_map/reduce_scatter | solution.py:254
  160.1 91.8 %reduce-scatter.5.cloned.1.call-start = ((), (), s32[]{:S(2)}) async-start(), calls=%async_computation.6 | async-start | bytes 2621440 | tf_op jit(solution)/shard_map/reduce_scatter | solution.py:254
Sparse Core Ops, SparseCore 0:
  10.2 88.6 all-gather.7
  100.5 52.9 all-gather.5
  160.2 46.6 reduce-scatter.2
  209.1 42.8 reduce-scatter.4
where the time goes:
time: 262 us; the launch traced here: 261 us
  waiting for transfers between devices  127 us (48%)
  Pallas kernels  53.8 us (21%)
  blocking collectives  44.3 us (17%)
  local copies, waits for them, and re-layouts  13.8 us (5%)
  between operations  13.2 us (5%)
  starting transfers between devices  4.68 us (2%)
  other arithmetic  3.78 us (1%)
    all_gather x1, waiting for transfers between devices, body(): gathered = lax.all_gather(packed, ('span', 'head'), axis=0, tiled=False)  62.2 us
    reduce_scatter x2, waiting for transfers between devices, body(): lax.psum_scatter(partial, 'head', scatter_dimension=1, tiled=True)  58.2 us
    all_gather x2, blocking collectives, body(): every = lax.all_gather(lse, 'head', axis=0, tiled=False)  34.6 us
    pallas_call x2, Pallas kernels, grouped_matmul(): pl.pallas_call(matmul_kernel, out_shape=jax.ShapeDtypeStruct((rows, group...  21.7 us
    pallas_call x2, Pallas kernels, attend(): pl.pallas_call(functools.partial(attend_kernel, spans=spans, neighbors=ne...  18.9 us
    pallas_call x2, Pallas kernels, project(): pl.pallas_call(project_kernel, out_shape=jax.ShapeDtypeStruct((rows, w.sh...  13.2 us
    all_to_all x1, blocking collectives, body(): lax.all_to_all(request, 'span', split_axis=0, concat_axis=0, tiled=True)  9.69 us
    all_gather x1, waiting for transfers between devices, body(): out_all = lax.all_gather(late_out, 'head', axis=0, tiled=True)  6.23 us
  transfers between devices with their start and end apart: 5, of which 4 were waited for; matrix products, arithmetic and copies ran while one was open for 5% of the time, Pallas kernels for 18%

commit v1 on v0

v1 whole, which is shorter than its diff:
```python
import functools

import jax
import jax.numpy as jnp
from jax import lax
from jax.experimental import pallas as pl
from jax.experimental.pallas import tpu as pltpu
from jax.sharding import PartitionSpec as P

HEAD_DIM = 64
SPAN_LEN = 64
SEQ_LEN = 2048
VMEM = 63 * 1024 * 1024
CHUNK_SPANS = 4
LINK = pl.DeviceIdType.MESH


def flip(index, bits, size):
    out = 0
    weight = 1
    while weight < size:
        out = out + weight * ((index // weight + bits // weight) % 2)
        weight *= 2
    return out


def kernel(
    span_size,
    head_size,
    position_ref,
    request_ref,
    states_hbm,
    encodings_hbm,
    query_hbm,
    key_hbm,
    value_hbm,
    out_hbm,
    o_ref,
    enc,
    sent,
    arrived,
    weights,
    outs,
    states,
    queries,
    kv,
    own,
    right,
    left,
    lse,
    top,
    ctx,
    score,
    expo,
    final,
    asked,
    asked_s,
    local_sem,
    ask_send,
    ask_recv,
    enc_send,
    enc_recv,
    line_send,
    line_recv,
    pair_send,
    pair_recv,
    lse_send,
    lse_recv,
    right_send,
    right_recv,
    left_send,
    left_recv,
):
    me = lax.axis_index("span")
    plane = lax.axis_index("head")
    core = me % 2
    partner = me + 1 - 2 * core
    slots, tokens, model = encodings_hbm.shape
    per_peer = kv.shape[1] // span_size
    group = query_hbm.shape[1]
    last = head_size - 1

    own_copies = [
        pltpu.make_async_copy(key_hbm, weights.at[plane, :, 0:group], local_sem.at[0]),
        pltpu.make_async_copy(value_hbm, weights.at[plane, :, group : 2 * group], local_sem.at[1]),
        pltpu.make_async_copy(query_hbm, weights.at[plane, :, 2 * group : 3 * group], local_sem.at[2]),
        pltpu.make_async_copy(encodings_hbm, enc, local_sem.at[3]),
        pltpu.make_async_copy(states_hbm, states, local_sem.at[4]),
        pltpu.make_async_copy(out_hbm, outs.at[plane], local_sem.at[5]),
    ]
    for copy in own_copies:
        copy.start()
    asked[me] = request_ref[me]

    barrier = pltpu.get_barrier_semaphore()
    for k in range(1, span_size):
        pl.semaphore_signal(
            barrier, inc=1, device_id=(flip(me, k, span_size), plane), device_id_type=LINK
        )
    for k in range(1, head_size):
        pl.semaphore_signal(
            barrier, inc=1, device_id=(me, (plane + k) % head_size), device_id_type=LINK
        )
    pl.semaphore_wait(barrier, span_size + head_size - 2)

    def ask(k):
        peer = flip(me, k, span_size)
        return pltpu.make_async_remote_copy(
            src_ref=request_ref.at[peer],
            dst_ref=asked.at[me],
            send_sem=ask_send.at[k],
            recv_sem=ask_recv.at[k],
            device_id=(peer, plane),
            device_id_type=LINK,
        )

    def landed(k):
        peer = flip(me, k, span_size)
        return pltpu.make_async_remote_copy(
            src_ref=request_ref.at[peer],
            dst_ref=asked.at[peer],
            send_sem=ask_send.at[k],
            recv_sem=ask_recv.at[k],
            device_id=(peer, plane),
            device_id_type=LINK,
        )

    for k in range(1, span_size):
        ask(k).start()

    halves = ((weights, weights.shape[1] // 2, 0), (outs, outs.shape[1] // 2, 1))

    def line_copy(which, shard, to, direction):
        buf, half, slot = halves[which]
        rows = pl.ds(pl.multiple_of(core * half, half), half)
        return pltpu.make_async_remote_copy(
            src_ref=buf.at[shard, rows],
            dst_ref=buf.at[shard, rows],
            send_sem=line_send.at[slot, shard, direction],
            recv_sem=line_recv.at[slot, shard],
            device_id=(me, to),
            device_id_type=LINK,
        )

    def pair_copy(which, shard):
        buf, half, slot = halves[which]
        rows = pl.ds(pl.multiple_of(core * half, half), half)
        return pltpu.make_async_remote_copy(
            src_ref=buf.at[shard, rows],
            dst_ref=buf.at[shard, rows],
            send_sem=pair_send.at[slot, shard],
            recv_sem=pair_recv.at[slot, shard],
            device_id=(partner, plane),
            device_id_type=LINK,
        )

    def pair_landed(which, shard):
        buf, half, slot = halves[which]
        rows = pl.ds(pl.multiple_of((1 - core) * half, half), half)
        return pltpu.make_async_remote_copy(
            src_ref=buf.at[shard, rows],
            dst_ref=buf.at[shard, rows],
            send_sem=pair_send.at[slot, shard],
            recv_sem=pair_recv.at[slot, shard],
            device_id=(partner, plane),
            device_id_type=LINK,
        )

    def send_own(which):
        @pl.when(plane < last)
        def _():
            line_copy(which, plane, plane + 1, 0).start()

        @pl.when(plane > 0)
        def _():
            line_copy(which, plane, plane - 1, 1).start()

    def pass_on(which, k):
        @pl.when(plane - k >= 0)
        def _():
            shard = plane - k
            line_copy(which, shard, plane, 0).wait_recv()

            @pl.when(plane < last)
            def _():
                line_copy(which, shard, plane + 1, 0).start()

            pair_copy(which, shard).start()

        @pl.when(plane + k <= last)
        def _():
            shard = plane + k
            line_copy(which, shard, plane, 1).wait_recv()

            @pl.when(plane > 0)
            def _():
                line_copy(which, shard, plane - 1, 1).start()

            pair_copy(which, shard).start()

    for copy in own_copies[:3]:
        copy.wait()
    send_own(0)

    for k in range(1, span_size):
        landed(k).wait_recv()
    to_scalar = pltpu.make_async_copy(asked, asked_s, local_sem.at[6])
    to_scalar.start()
    own_copies[3].wait()
    to_scalar.wait()

    def enc_copy(k):
        peer = flip(me, k, span_size)
        return pltpu.make_async_remote_copy(
            src_ref=sent.at[peer],
            dst_ref=arrived.at[me],
            send_sem=enc_send.at[k],
            recv_sem=enc_recv.at[k],
            device_id=(peer, plane),
            device_id_type=LINK,
        )

    def enc_landed(k):
        peer = flip(me, k, span_size)
        return pltpu.make_async_remote_copy(
            src_ref=sent.at[peer],
            dst_ref=arrived.at[peer],
            send_sem=enc_send.at[k],
            recv_sem=enc_recv.at[k],
            device_id=(peer, plane),
            device_id_type=LINK,
        )

    def pick(buf, peer):
        for j in range(per_peer):
            buf[peer, j] = enc[asked_s[peer, 0, j]]

    def pick_and_send(k, carry):
        pick(sent, flip(me, k, span_size))

        @pl.when(k > 1)
        def _():
            enc_copy(k - 1).start()

        return carry

    lax.fori_loop(1, span_size, pick_and_send, 0)
    pick(arrived, me)
    enc_copy(span_size - 1).start()

    own_copies[4].wait()
    blocks, block_len, _ = states.shape
    blocks_seq = SEQ_LEN // block_len
    row = lax.broadcasted_iota(jnp.int32, (block_len, model), 0)

    def move_up(b, carry):
        inside = (b + 1) % blocks_seq != 0
        following = states[(b + 1) % blocks].astype(jnp.float32)
        following = jnp.where(inside, following, 0.0)
        tail = states[b].astype(jnp.float32)[block_len - 1 :]
        moved = jnp.where(row == 0, tail, pltpu.roll(following, 1, 0))
        states[b] = moved.astype(states.dtype)
        return carry

    lax.fori_loop(0, blocks, move_up, 0)

    def project_queries(shard):
        step = min(4, blocks)

        def one(b, carry):
            x = states[pl.ds(b * step, step)].reshape(step * block_len, model)
            y = jnp.dot(
                x, weights[shard, :, 2 * group : 3 * group], preferred_element_type=jnp.float32
            )
            queries[shard, pl.ds(b * step, step)] = y.astype(queries.dtype).reshape(
                step, block_len, group
            )
            return carry

        lax.fori_loop(0, blocks // step, one, 0)

    def project_keys(shard, first, end):
        def one(k, carry):
            peer = flip(me, k, span_size)
            x = arrived[peer].reshape(per_peer * tokens, model)
            y = jnp.dot(x, weights[shard, :, 0 : 2 * group], preferred_element_type=jnp.float32)
            kv[shard, pl.ds(peer * per_peer, per_peer)] = y.astype(kv.dtype).reshape(
                per_peer, tokens, 2 * group
            )
            return carry

        lax.fori_loop(first, end, one, 0)

    def shards_at(k, work):
        if k == 0:
            work(plane)
            return

        @pl.when(plane - k >= 0)
        def _():
            work(plane - k)

        @pl.when(plane + k <= last)
        def _():
            work(plane + k)

    near, mid = span_size // 4, span_size - span_size // 4
    bounds = (0, near, mid, span_size)

    def keys_of(k, a, b):
        shards_at(k, lambda shard: project_keys(shard, bounds[a], bounds[b]))

    def wait_enc(a):
        for k in range(max(bounds[a], 1), bounds[a + 1]):
            enc_landed(k).wait_recv()

    def wait_pair(which, k):
        shards_at(k, lambda shard: pair_landed(which, shard).wait_recv())

    project_queries(plane)
    wait_enc(0)
    keys_of(0, 0, 1)
    for k in range(1, last):
        pass_on(0, k)
        if k == last - 1:
            own_copies[5].wait()
            send_own(1)
        wait_pair(0, k)
        shards_at(k, project_queries)
        keys_of(k, 0, 1)
        if k == 1:
            wait_enc(1)
            keys_of(0, 1, 2)
            keys_of(1, 1, 2)
        else:
            keys_of(k, 1, 2)
    wait_enc(2)
    for k in range(last):
        keys_of(k, 2, 3)
    pass_on(0, last)
    wait_pair(0, last)
    shards_at(last, project_queries)
    keys_of(last, 0, 3)
    for k in range(1, head_size):
        pass_on(1, k)
    for k in range(1, head_size):
        wait_pair(1, k)

    chunks = right.shape[0]
    chunk_spans = CHUNK_SPANS
    heads = head_size * group // HEAD_DIM
    neighbors = position_ref.shape[0] // blocks
    keys = neighbors * tokens
    packed = group // HEAD_DIM
    wide = packed * keys
    diagonal = (
        lax.broadcasted_iota(jnp.int32, (wide, group), 0) // keys
        == lax.broadcasted_iota(jnp.int32, (wide, group), 1) // HEAD_DIM
    )
    pair = 128 // keys
    lane = lax.broadcasted_iota(jnp.int32, (SPAN_LEN, 128), 1)
    lane_head = lane // keys
    collect = (
        lax.broadcasted_iota(jnp.int32, (heads * keys, 128), 0) // keys
        == lax.broadcasted_iota(jnp.int32, (heads * keys, 128), 1)
    ).astype(jnp.bfloat16)

    def attend(chunk):
        def widened(c, g, base):
            part = jnp.concatenate(
                [
                    kv[g, position_ref[(chunk * chunk_spans + c) * neighbors + n]][
                        :, base : base + group
                    ]
                    for n in range(neighbors)
                ],
                axis=0,
            )
            return jnp.where(diagonal, jnp.concatenate([part] * packed, axis=0), 0)

        for c in range(chunk_spans):
            rows = slice(c * SPAN_LEN, (c + 1) * SPAN_LEN)
            for g in range(head_size):
                score[rows, g * wide : (g + 1) * wide] = lax.dot_general(
                    queries[g, chunk * chunk_spans + c],
                    widened(c, g, 0),
                    (((1,), (1,)), ((), ())),
                    preferred_element_type=jnp.float32,
                ) * (HEAD_DIM ** (-0.5))
        tops = []
        for c in range(chunk_spans):
            rows = slice(c * SPAN_LEN, (c + 1) * SPAN_LEN)
            top_all = jnp.zeros((SPAN_LEN, 128), jnp.float32)
            for t in range(heads // pair):
                s = score[rows, t * 128 : (t + 1) * 128]
                peak = None
                for n in range(pair):
                    m = jnp.max(jnp.where(lane_head == n, s, -jnp.inf), axis=1, keepdims=True)
                    peak = m if peak is None else jnp.where(lane_head == n, m, peak)
                    top_all = jnp.where(lane == t * pair + n, m, top_all)
                expo[rows, t * 128 : (t + 1) * 128] = jnp.exp(s - peak).astype(jnp.bfloat16)
            tops.append(top_all)
        top_all = jnp.concatenate(tops, axis=0)
        total = jnp.dot(expo[...], collect, preferred_element_type=jnp.float32)
        top_rows = top_all.T[:heads]
        top[chunk % 2] = top_rows
        lse[plane, chunk] = top_rows + jnp.log(total.T[:heads])
        for c in range(chunk_spans):
            rows = slice(c * SPAN_LEN, (c + 1) * SPAN_LEN)
            for g in range(head_size):
                ctx[chunk % 2, rows, g * group : (g + 1) * group] = jnp.dot(
                    expo[rows, g * wide : (g + 1) * wide],
                    widened(c, g, group),
                    preferred_element_type=jnp.float32,
                ).astype(ctx.dtype)

    def lse_copy(chunk, k):
        return pltpu.make_async_remote_copy(
            src_ref=lse.at[plane, chunk],
            dst_ref=lse.at[plane, chunk],
            send_sem=lse_send.at[chunk, k],
            recv_sem=lse_recv.at[chunk, k],
            device_id=(me, (plane + k) % head_size),
            device_id_type=LINK,
        )

    def lse_landed(chunk, k):
        origin = (plane + head_size - k) % head_size
        return pltpu.make_async_remote_copy(
            src_ref=lse.at[origin, chunk],
            dst_ref=lse.at[origin, chunk],
            send_sem=lse_send.at[chunk, k],
            recv_sem=lse_recv.at[chunk, k],
            device_id=(me, (plane + k) % head_size),
            device_id_type=LINK,
        )

    def project(chunk):
        every = lse[:, chunk]
        highest = jnp.max(every, axis=0)
        total = jnp.sum(jnp.exp(every - highest[None]), axis=0)
        scale = jnp.exp(top[chunk % 2] - highest) / total
        high = scale.astype(jnp.bfloat16)
        low = (scale - high.astype(jnp.float32)).astype(jnp.bfloat16)
        spread = (
            lax.broadcasted_iota(jnp.int32, (2 * heads, model), 0) % heads
            == lax.broadcasted_iota(jnp.int32, (2 * heads, model), 1) // HEAD_DIM
        ).astype(jnp.bfloat16)
        factor = lax.dot_general(
            jnp.concatenate([high, low], axis=0),
            spread,
            (((0,), (0,)), ((), ())),
            preferred_element_type=jnp.float32,
        )
        scaled = (ctx[chunk % 2].astype(jnp.float32) * factor).astype(jnp.bfloat16)
        w = outs[...].reshape(head_size * group, model)
        y = jnp.dot(scaled, w, preferred_element_type=jnp.float32)
        for q in range(head_size):
            own[chunk % head_size, q] = y[:, q * group : (q + 1) * group]

    def right_copy(chunk, q, to):
        return pltpu.make_async_remote_copy(
            src_ref=right.at[chunk, q],
            dst_ref=right.at[chunk, q],
            send_sem=right_send.at[chunk, q],
            recv_sem=right_recv.at[chunk, q],
            device_id=(me, to),
            device_id_type=LINK,
        )

    def left_copy(chunk, q, to):
        return pltpu.make_async_remote_copy(
            src_ref=left.at[chunk, q],
            dst_ref=left.at[chunk, q],
            send_sem=left_send.at[chunk, q],
            recv_sem=left_recv.at[chunk, q],
            device_id=(me, to),
            device_id_type=LINK,
        )

    def step(it, carry):
        @pl.when(it < chunks)
        def _():
            attend(it)
            for k in range(1, head_size):
                lse_copy(it, k).start()

        @pl.when((it >= 1) & (it <= chunks))
        def _():
            for k in range(1, head_size):
                lse_landed(it - 1, k).wait_recv()
            project(it - 1)

        to_right = it - 1 - plane
        right_on = (to_right >= 0) & (to_right < chunks)
        to_left = it - 1 - (last - plane)
        left_on = (to_left >= 0) & (to_left < chunks)
        for q in range(head_size):

            @pl.when(right_on & (q > plane) & (plane == 0))
            def _():
                right[to_right, q] = own[to_right % head_size, q].astype(right.dtype)

            @pl.when(right_on & (q > plane) & (plane > 0))
            def _():
                right_copy(to_right, q, plane).wait_recv()
                right[to_right, q] = (
                    own[to_right % head_size, q] + right[to_right, q].astype(jnp.float32)
                ).astype(right.dtype)

            @pl.when(left_on & (q < plane) & (plane == last))
            def _():
                left[to_left, q] = own[to_left % head_size, q].astype(left.dtype)

            @pl.when(left_on & (q < plane) & (plane < last))
            def _():
                left_copy(to_left, q, plane).wait_recv()
                left[to_left, q] = (
                    own[to_left % head_size, q] + left[to_left, q].astype(jnp.float32)
                ).astype(left.dtype)

        for q in range(head_size):

            @pl.when(right_on & (q > plane))
            def _():
                right_copy(to_right, q, plane + 1).start()

            @pl.when(left_on & (q < plane))
            def _():
                left_copy(to_left, q, plane - 1).start()

        done = it - 1 - jnp.maximum(plane, last - plane)

        @pl.when((done >= 0) & (done < chunks))
        def _():
            @pl.when(plane == 0)
            def _():
                left_copy(done, plane, plane).wait_recv()
                put(done, own[done % head_size, plane] + left[done, plane].astype(jnp.float32))

            @pl.when(plane == last)
            def _():
                right_copy(done, plane, plane).wait_recv()
                put(done, own[done % head_size, plane] + right[done, plane].astype(jnp.float32))

            @pl.when((plane > 0) & (plane < last))
            def _():
                left_copy(done, plane, plane).wait_recv()
                right_copy(done, plane, plane).wait_recv()
                put(
                    done,
                    own[done % head_size, plane]
                    + left[done, plane].astype(jnp.float32)
                    + right[done, plane].astype(jnp.float32),
                )

        return carry

    def put(chunk, value):
        final[pl.ds(chunk * chunk_spans, chunk_spans)] = value.reshape(
            chunk_spans, SPAN_LEN, group
        )

    lax.fori_loop(0, chunks + head_size, step, 0)

    out_row = lax.broadcasted_iota(jnp.int32, (SPAN_LEN, group), 0)

    def move_down(b, carry):
        before = jnp.where(b % blocks_seq != 0, final[(b + blocks - 1) % blocks], 0.0)
        moved = jnp.where(
            out_row == SPAN_LEN - 1, final[b][0:1], pltpu.roll(before, SPAN_LEN - 1, 0)
        )
        o_ref[b] = moved.astype(o_ref.dtype)
        return carry

    lax.fori_loop(0, blocks, move_down, 0)

    for k in range(1, span_size):
        ask(k).wait_send()
        enc_copy(k).wait_send()
    for which in range(2):

        @pl.when(plane < last)
        def _():
            line_copy(which, plane, plane + 1, 0).wait_send()

        @pl.when(plane > 0)
        def _():
            line_copy(which, plane, plane - 1, 1).wait_send()

        for k in range(1, head_size):

            @pl.when(plane - k >= 0)
            def _():
                @pl.when(plane < last)
                def _():
                    line_copy(which, plane - k, plane + 1, 0).wait_send()

                pair_copy(which, plane - k).wait_send()

            @pl.when(plane + k <= last)
            def _():
                @pl.when(plane > 0)
                def _():
                    line_copy(which, plane + k, plane - 1, 1).wait_send()

                pair_copy(which, plane + k).wait_send()

    def drain(chunk, carry):
        for k in range(1, head_size):
            lse_copy(chunk, k).wait_send()
        for q in range(head_size):

            @pl.when(q > plane)
            def _():
                right_copy(chunk, q, plane + 1).wait_send()

            @pl.when(q < plane)
            def _():
                left_copy(chunk, q, plane - 1).wait_send()

        return carry

    lax.fori_loop(0, chunks, drain, 0)


def fused(
    position, request, states, encodings, query_weight, key_weight, value_weight, out_weight
):
    span_size = lax.axis_size("span")
    head_size = lax.axis_size("head")
    slots, tokens, model = encodings.shape
    rows = states.shape[0]
    group = query_weight.shape[1]
    entries = position.shape[0]
    per_peer = entries // span_size
    blocks = rows // SPAN_LEN
    chunks = blocks // CHUNK_SPANS
    chunk_rows = CHUNK_SPANS * SPAN_LEN
    heads = head_size * group // HEAD_DIM
    score_cols = heads * (entries // blocks) * tokens
    bf16, f32 = jnp.bfloat16, jnp.float32
    dma = pltpu.SemaphoreType.DMA
    vmem = pl.BlockSpec(memory_space=pltpu.VMEM)
    hbm = pl.BlockSpec(memory_space=pl.ANY)
    return pl.pallas_call(
        functools.partial(kernel, span_size, head_size),
        out_shape=jax.ShapeDtypeStruct((blocks, SPAN_LEN, group), bf16),
        in_specs=[pl.BlockSpec(memory_space=pltpu.SMEM), vmem] + [hbm] * 6,
        out_specs=vmem,
        scratch_shapes=[
            pltpu.VMEM((slots, tokens, model), bf16),
            pltpu.VMEM((span_size, per_peer, tokens, model), bf16),
            pltpu.VMEM((span_size, per_peer, tokens, model), bf16),
            pltpu.VMEM((head_size, model, 3 * group), bf16),
            pltpu.VMEM((head_size, group, model), bf16),
            pltpu.VMEM((blocks, SPAN_LEN, model), bf16),
            pltpu.VMEM((head_size, blocks, SPAN_LEN, group), bf16),
            pltpu.VMEM((head_size, entries, tokens, 2 * group), bf16),
            pltpu.VMEM((head_size, head_size, chunk_rows, group), f32),
            pltpu.VMEM((chunks, head_size, chunk_rows, group), bf16),
            pltpu.VMEM((chunks, head_size, chunk_rows, group), bf16),
            pltpu.VMEM((head_size, chunks, heads, chunk_rows), f32),
            pltpu.VMEM((2, heads, chunk_rows), f32),
            pltpu.VMEM((2, chunk_rows, model), bf16),
            pltpu.VMEM((chunk_rows, score_cols), f32),
            pltpu.VMEM((chunk_rows, score_cols), bf16),
            pltpu.VMEM((blocks, SPAN_LEN, group), f32),
            pltpu.VMEM(request.shape, jnp.int32),
            pltpu.SMEM(request.shape, jnp.int32),
            dma((7,)),
            dma((span_size,)),
            dma((span_size,)),
            dma((span_size,)),
            dma((span_size,)),
            dma((2, head_size, 2)),
            dma((2, head_size)),
            dma((2, head_size)),
            dma((2, head_size)),
            dma((chunks, head_size)),
            dma((chunks, head_size)),
            dma((chunks, head_size)),
            dma((chunks, head_size)),
            dma((chunks, head_size)),
            dma((chunks, head_size)),
        ],
        compiler_params=pltpu.CompilerParams(
            collective_id=0, has_side_effects=True, vmem_limit_bytes=VMEM
        ),
        cost_estimate=pl.CostEstimate(
            flops=6 * rows * model * head_size * group, bytes_accessed=16 << 20, transcendentals=0
        ),
    )(
        position,
        request,
        states.reshape(blocks, SPAN_LEN, model),
        encodings,
        query_weight,
        key_weight,
        value_weight,
        out_weight,
    )


def body(
    decoder_states, encodings, neighbor_table, query_weight, key_weight, value_weight, out_weight
):
    peer_count = lax.axis_size("span")
    shard_ids = neighbor_table[:, :, 0].reshape(-1)
    slot_ids = neighbor_table[:, :, 1].reshape(-1)
    entries = shard_ids.shape[0]
    per_peer = entries // peer_count
    numbering = jnp.arange(entries, dtype=jnp.int32)
    same_before = (shard_ids[:, None] == shard_ids[None, :]) & (
        numbering[None, :] < numbering[:, None]
    )
    ranking = jnp.sum(same_before.astype(jnp.int32), axis=1)
    position = shard_ids * per_peer + ranking
    placed = position[None, :] == numbering[:, None]
    request = jnp.sum(jnp.where(placed, slot_ids[None, :], 0), axis=1)
    request = request.reshape(peer_count, 1, per_peer)
    request = jnp.pad(request, ((0, 0), (0, 7), (0, 128 - per_peer)))
    out = fused(
        position,
        request,
        decoder_states,
        encodings,
        query_weight,
        key_weight,
        value_weight,
        out_weight,
    )
    return out.reshape(decoder_states.shape[0], -1)


def solution(mesh):
    return jax.shard_map(
        body,
        mesh=mesh,
        in_specs=(
            P("span", None),
            P("span", "head", None),
            P("span", None, None),
            P(None, "head"),
            P(None, "head"),
            P(None, "head"),
            P("head", None),
        ),
        out_specs=P("span", "head"),
        check_vma=False,
    )
```

time: 262 us -> 187 us (0.71)
  Pallas kernels: 53.8 us -> 181 us
  waiting for transfers between devices: 127 us -> 0 us
  blocking collectives: 44.3 us -> 0 us
  between operations: 13.2 us -> 0.04 us
  local copies, waits for them, and re-layouts: 13.8 us -> 4.13 us
  starting transfers between devices: 4.68 us -> 0 us
  other arithmetic: 3.78 us -> 0.29 us
    pallas_call x6 -> x1, Pallas kernels: 53.8 us -> 181 us  [fused(): pl.pallas_call(functools.partial(kernel, span_size, head_size), out_shape...]
    all_gather x2 -> x0, waiting for transfers between devices: 68.4 us -> none  [the longest x1 62.2 us: body(): gathered = lax.all_gather(packed, ('span', 'head'), axis=0, tiled=False)]
    reduce_scatter x2 -> x0, waiting for transfers between devices: 58.2 us -> none  [body(): lax.psum_scatter(partial, 'head', scatter_dimension=1, tiled=True)]
    all_gather x2 -> x0, blocking collectives: 34.6 us -> none  [body(): every = lax.all_gather(lse, 'head', axis=0, tiled=False)]
    all_to_all x1 -> x0, blocking collectives: 9.69 us -> none  [body(): lax.all_to_all(request, 'span', split_axis=0, concat_axis=0, tiled=True)]
    gather x1 -> x0, local copies, waits for them, and re-layouts: 5.05 us -> none  [body(): selected = encodings[wanted]]
    all_to_all x1 -> x0, starting transfers between devices: 4.55 us -> none  [body(): lax.all_to_all(selected, 'span', split_axis=0, concat_axis=0, tiled=True)]
    reshape x2 -> x1, local copies, waits for them, and re-layouts: 3.61 us -> 0.08 us  [body(): request = request.reshape(peer_count, 1, per_peer)]
  transfers between devices with their start and end apart: 5 -> 0, of which waited for: 4 -> 0; matrix products, arithmetic and copies ran while one was open for 5% -> 0% of each run, Pallas kernels for 18% -> 0%
where the time goes in v1:
time: 187 us; the launch traced here: 186 us
  Pallas kernels  181 us (97%)
  local copies, waits for them, and re-layouts  4.13 us (2%)
    pallas_call x1, Pallas kernels, fused(): pl.pallas_call(functools.partial(kernel, span_size, head_size), out_shape...  181 us

profile of v1, /device:TPU:0, one launch (start us, length us, event | category | flops | bytes accessed | tf_op | source)
XLA Modules:
  0.0 185.8 jit_solution(16868662123951380829)
XLA Ops:
  0.0 0.8 fusion.1
  0.8 0.1 copy.15
  0.9 0.1 broadcast_in_dim.18
  1.0 0.1 copy.14
  1.0 0.1 reshape_squeeze.3
  1.2 0.2 convert_reduce_fusion
  1.3 0.0 copy-start
  1.4 0.1 select_reduce_fusion
  1.5 0.1 reshape.20
  1.5 0.6 pad.4.request_ref
  2.2 0.0 copy-done
  2.2 181.3 %shard_map.73 = bf16[32,64,256]{2,1,0:T(8,128)(2,1)} custom-call(s32[64]{0:T(128)} %copy-done, s32[8,8,128]{2,1,0:T(8,128)} %pad.4.request_ref, bf16[32,64,1024]{2,1,0:T(8,128)(2,1)} %bitcast.9, bf16[64,32,1024]{2,1,0:T(8,128)(2,1)} %encodings_hbm.1, bf16[1024,256]{1,0:T(8,128)(2,1)} %query_hbm.1, bf16[1024,256]{1,0:T(8,128)(2,1)} %key_hbm.1, ...), custom_call_target="tpu_custom_call" | custom-call | flops 12884901888 | bytes 16777216 | tf_op jit(solution)/shard_map/pallas_call | solution.py:646
  183.5 2.3 %copy.18 = bf16[2048,256]{1,0:T(8,128)(2,1)} copy(bf16[2048,256]{1,0:T(8,128)(2,1)} %bitcast.7) | data formatting | bytes 2097152
  (1 shorter events, 0.0 us)
Async XLA Ops:
  1.3 0.8 copy-start

commit v2 on v1

--- a/solution.py
+++ b/solution.py
@@ -27,7 +27,10 @@
 def kernel(
     span_size,
     head_size,
+    rows_a,
     position_ref,
+    order_ref,
+    place_ref,
     request_ref,
     states_hbm,
     encodings_hbm,
@@ -38,12 +41,16 @@
     o_ref,
     enc,
     sent,
-    arrived,
+    arrived_a,
+    arrived_b,
+    arrived_c,
     weights,
     outs,
     states,
     queries,
-    kv,
+    kv_a,
+    kv_b,
+    kv_c,
     own,
     right,
     left,
@@ -60,8 +67,12 @@
     ask_recv,
     enc_send,
     enc_recv,
+    relay_send,
+    relay_recv,
     line_send,
     line_recv,
+    piece_send,
+    piece_recv,
     pair_send,
     pair_recv,
     lse_send,
@@ -74,11 +85,14 @@
     me = lax.axis_index("span")
     plane = lax.axis_index("head")
     core = me % 2
+    last = head_size - 1
     partner = me + 1 - 2 * core
     slots, tokens, model = encodings_hbm.shape
-    per_peer = kv.shape[1] // span_size
+    per_peer = sent.shape[1]
+    rows_b = per_peer - rows_a
+    split = rows_b > 0
+    middle = (plane > 0) & (plane < last)
     group = query_hbm.shape[1]
-    last = head_size - 1
 
     own_copies = [
         pltpu.make_async_copy(key_hbm, weights.at[plane, :, 0:group], local_sem.at[0]),
@@ -142,6 +156,54 @@
             device_id_type=LINK,
         )
 
+    bit_x, bit_y = (me // 2) % 2, (me // 4) % 2
+    quarter = weights.shape[1] // 8
+
+    def piece_copy(shard, piece, slot, to_span, to_plane):
+        rows = pl.ds(pl.multiple_of(core * 4 * quarter + piece * quarter, quarter), quarter)
+        return pltpu.make_async_remote_copy(
+            src_ref=weights.at[shard, rows],
+            dst_ref=weights.at[shard, rows],
+            send_sem=piece_send.at[slot],
+            recv_sem=piece_recv.at[slot],
+            device_id=(to_span, to_plane),
+            device_id_type=LINK,
+        )
+
+    def end_pieces(shard, to_plane):
+        return (
+            piece_copy(shard, 1 - bit_x, 0, me, to_plane),
+            piece_copy(shard, 3 - bit_y, 1, me, to_plane),
+        )
+
+    def shared_pieces(shard):
+        return (
+            piece_copy(shard, 1 - bit_x, 2, flip(me, 2, span_size), plane),
+            piece_copy(shard, 3 - bit_y, 3, flip(me, 4, span_size), plane),
+        )
+
+    def shared_landed(shard):
+        return (
+            piece_copy(shard, bit_x, 2, flip(me, 2, span_size), plane),
+            piece_copy(shard, 2 + bit_y, 3, flip(me, 4, span_size), plane),
+        )
+
+    def far_shard(work):
+        @pl.when((plane == 0) | (plane == last))
+        def _():
+            work(last - plane)
+
+    def far_arrives(shard):
+        for copy in end_pieces(shard, plane):
+            copy.wait_recv()
+        for copy in shared_pieces(shard):
+            copy.start()
+
+    def far_shared(shard):
+        for copy in shared_landed(shard):
+            copy.wait_recv()
+        pair_copy(0, shard).start()
+
     def pair_copy(which, shard):
         buf, half, slot = halves[which]
         rows = pl.ds(pl.multiple_of(core * half, half), half)
@@ -175,15 +237,25 @@
         def _():
             line_copy(which, plane, plane - 1, 1).start()
 
+    def whole_hop(which, shard, to):
+        if which == 1:
+            return plane >= 0
+        return (shard - to != last) & (to - shard != last)
+
     def pass_on(which, k):
         @pl.when(plane - k >= 0)
         def _():
             shard = plane - k
             line_copy(which, shard, plane, 0).wait_recv()
 
-            @pl.when(plane < last)
+            @pl.when((plane < last) & whole_hop(which, shard, plane + 1))
             def _():
                 line_copy(which, shard, plane + 1, 0).start()
+
+            @pl.when((plane < last) & ~whole_hop(which, shard, plane + 1))
+            def _():
+                for copy in end_pieces(shard, plane + 1):
+                    copy.start()
 
             pair_copy(which, shard).start()
 
@@ -192,15 +264,26 @@
             shard = plane + k
             line_copy(which, shard, plane, 1).wait_recv()
 
-            @pl.when(plane > 0)
+            @pl.when((plane > 0) & whole_hop(which, shard, plane - 1))
             def _():
                 line_copy(which, shard, plane - 1, 1).start()
+
+            @pl.when((plane > 0) & ~whole_hop(which, shard, plane - 1))
+            def _():
+                for copy in end_pieces(shard, plane - 1):
+                    copy.start()
 
             pair_copy(which, shard).start()
 
     for copy in own_copies[:3]:
         copy.wait()
     send_own(0)
+    own_copies[5].wait()
+
+    @pl.when(~middle)
+    def _():
+        send_own(1)
+
 
     for k in range(1, span_size):
         landed(k).wait_recv()
@@ -209,44 +292,67 @@
     own_copies[3].wait()
     to_scalar.wait()
 
-    def enc_copy(k):
+    def enc_copy(k, part):
         peer = flip(me, k, span_size)
-        return pltpu.make_async_remote_copy(
-            src_ref=sent.at[peer],
-            dst_ref=arrived.at[me],
-            send_sem=enc_send.at[k],
-            recv_sem=enc_recv.at[k],
+        if part == 0:
+            src, dst = sent.at[peer, pl.ds(0, rows_a)], arrived_a.at[me]
+        else:
+            src, dst = sent.at[peer, pl.ds(rows_a, rows_b)], arrived_b.at[me]
+        return pltpu.make_async_remote_copy(
+            src_ref=src,
+            dst_ref=dst,
+            send_sem=enc_send.at[part, k],
+            recv_sem=enc_recv.at[part, k],
             device_id=(peer, plane),
             device_id_type=LINK,
         )
 
-    def enc_landed(k):
+    def enc_landed(k, part):
         peer = flip(me, k, span_size)
-        return pltpu.make_async_remote_copy(
-            src_ref=sent.at[peer],
-            dst_ref=arrived.at[peer],
-            send_sem=enc_send.at[k],
-            recv_sem=enc_recv.at[k],
+        dst = (arrived_a, arrived_b)[part].at[peer]
+        return pltpu.make_async_remote_copy(
+            src_ref=dst,
+            dst_ref=dst,
+            send_sem=enc_send.at[part, k],
+            recv_sem=enc_recv.at[part, k],
             device_id=(peer, plane),
             device_id_type=LINK,
         )
 
-    def pick(buf, peer):
-        for j in range(per_peer):
-            buf[peer, j] = enc[asked_s[peer, 0, j]]
-
-    def pick_and_send(k, carry):
-        pick(sent, flip(me, k, span_size))
-
-        @pl.when(k > 1)
-        def _():
-            enc_copy(k - 1).start()
-
-        return carry
-
-    lax.fori_loop(1, span_size, pick_and_send, 0)
-    pick(arrived, me)
-    enc_copy(span_size - 1).start()
+    mate = jnp.where(plane == 0, 1, last - 1)
+
+    def relay_copy(k):
+        peer = flip(me, k, span_size)
+        return pltpu.make_async_remote_copy(
+            src_ref=arrived_b.at[peer],
+            dst_ref=arrived_c.at[peer],
+            send_sem=relay_send.at[k],
+            recv_sem=relay_recv.at[k],
+            device_id=(me, mate),
+            device_id_type=LINK,
+        )
+
+    def pick(buf, peer, offset, begin, count):
+        for j in range(count):
+            buf[peer, offset + j] = enc[asked_s[peer, 0, begin + j]]
+
+    def pick_and_send(part, begin, count):
+        def one(k, carry):
+            pick(sent, flip(me, k, span_size), begin, begin, count)
+
+            @pl.when(k > 1)
+            def _():
+                enc_copy(k - 1, part).start()
+
+            return carry
+
+        lax.fori_loop(1, span_size, one, 0)
+        pick((arrived_a, arrived_b)[part], me, 0, begin, count)
+        enc_copy(span_size - 1, part).start()
+
+    if split:
+        pick_and_send(1, rows_a, rows_b)
+    pick_and_send(0, 0, rows_a)
 
     own_copies[4].wait()
     blocks, block_len, _ = states.shape
@@ -279,13 +385,15 @@
 
         lax.fori_loop(0, blocks // step, one, 0)
 
-    def project_keys(shard, first, end):
-        def one(k, carry):
-            peer = flip(me, k, span_size)
-            x = arrived[peer].reshape(per_peer * tokens, model)
+    def project_keys(shard, src, dst, first, end):
+        count = src.shape[1]
+
+        def one(chip, carry):
+            base = flip(me, 2 * chip, span_size) // 2 * 2
+            x = src[pl.ds(base, 2)].reshape(2 * count * tokens, model)
             y = jnp.dot(x, weights[shard, :, 0 : 2 * group], preferred_element_type=jnp.float32)
-            kv[shard, pl.ds(peer * per_peer, per_peer)] = y.astype(kv.dtype).reshape(
-                per_peer, tokens, 2 * group
+            dst[shard, pl.ds(base * count, 2 * count)] = y.astype(dst.dtype).reshape(
+                2 * count, tokens, 2 * group
             )
             return carry
 
@@ -304,75 +412,130 @@
         def _():
             work(plane + k)
 
-    near, mid = span_size // 4, span_size - span_size // 4
-    bounds = (0, near, mid, span_size)
-
-    def keys_of(k, a, b):
-        shards_at(k, lambda shard: project_keys(shard, bounds[a], bounds[b]))
-
-    def wait_enc(a):
-        for k in range(max(bounds[a], 1), bounds[a + 1]):
-            enc_landed(k).wait_recv()
+    chips = span_size // 2
+    near, far = chips // 4, chips - chips // 4
+
+    def keys_a(k, first, end):
+        shards_at(k, lambda shard: project_keys(shard, arrived_a, kv_a, first, end))
+
+    def keys_b(k, first, end):
+        shards_at(k, lambda shard: project_keys(shard, arrived_b, kv_b, first, end))
+
+    def keys_c(first, end):
+        for shard in range(head_size):
+            project_keys(shard, arrived_c, kv_c, first, end)
+
+    def wait_enc(part, first, end):
+        for k in range(max(2 * first, 1), 2 * end):
+            enc_landed(k, part).wait_recv()
+
+    def relay(first, end):
+        if split:
+
+            @pl.when(~middle)
+            def _():
+                wait_enc(1, first, end)
+                for k in range(2 * first, 2 * end):
+                    relay_copy(k).start()
+
+    def relayed(first, end):
+        for k in range(2 * first, 2 * end):
+            relay_copy(k).wait_recv()
 
     def wait_pair(which, k):
         shards_at(k, lambda shard: pair_landed(which, shard).wait_recv())
 
+    relay(0, near)
     project_queries(plane)
-    wait_enc(0)
-    keys_of(0, 0, 1)
+    wait_enc(0, 0, near)
+    keys_a(0, 0, near)
     for k in range(1, last):
         pass_on(0, k)
         if k == last - 1:
-            own_copies[5].wait()
-            send_own(1)
+
+            @pl.when(middle)
+            def _():
+                send_own(1)
+
         wait_pair(0, k)
         shards_at(k, project_queries)
-        keys_of(k, 0, 1)
+        keys_a(k, 0, near)
         if k == 1:
-            wait_enc(1)
-            keys_of(0, 1, 2)
-            keys_of(1, 1, 2)
-        else:
-            keys_of(k, 1, 2)
-    wait_enc(2)
+            relay(near, far)
+            relay(far, chips)
+    far_shard(far_arrives)
+    if split:
+        @pl.when(middle)
+        def _():
+            wait_enc(1, 0, chips)
+            for k in range(last):
+                keys_b(k, 0, chips)
+
+    wait_enc(0, near, far)
     for k in range(last):
-        keys_of(k, 2, 3)
-    pass_on(0, last)
+        keys_a(k, near, far)
+    @pl.when(middle)
+    def _():
+        for k in range(1, last):
+            pass_on(1, k)
+
+    wait_enc(0, far, chips)
+    for k in range(last):
+        keys_a(k, far, chips)
+    far_shard(far_shared)
     wait_pair(0, last)
     shards_at(last, project_queries)
-    keys_of(last, 0, 3)
-    for k in range(1, head_size):
-        pass_on(1, k)
+    keys_a(last, 0, chips)
+    @pl.when(~middle)
+    def _():
+        for k in range(1, last):
+            pass_on(1, k)
+
+    pass_on(1, last)
     for k in range(1, head_size):
         wait_pair(1, k)
-
-    chunks = right.shape[0]
+    if split:
+        @pl.when(middle)
+        def _():
+            relayed(0, far)
+            keys_c(0, far)
+
+
+    chunks = blocks // CHUNK_SPANS
     chunk_spans = CHUNK_SPANS
     heads = head_size * group // HEAD_DIM
     neighbors = position_ref.shape[0] // blocks
-    keys = neighbors * tokens
     packed = group // HEAD_DIM
-    wide = packed * keys
-    diagonal = (
-        lax.broadcasted_iota(jnp.int32, (wide, group), 0) // keys
-        == lax.broadcasted_iota(jnp.int32, (wide, group), 1) // HEAD_DIM
-    )
-    pair = 128 // keys
     lane = lax.broadcasted_iota(jnp.int32, (SPAN_LEN, 128), 1)
-    lane_head = lane // keys
-    collect = (
-        lax.broadcasted_iota(jnp.int32, (heads * keys, 128), 0) // keys
-        == lax.broadcasted_iota(jnp.int32, (heads * keys, 128), 1)
-    ).astype(jnp.bfloat16)
-
-    def attend(chunk):
+
+    def is_b(chunk):
+        if not split:
+            return chunk < 0
+        return ((chunk >= 2) & (chunk % 2 == 0)) | (chunk == chunks - 1)
+
+    def attend(chunk, sources):
+        keys = neighbors * len(sources) * tokens
+        wide = packed * keys
+        cols = heads * keys
+        pair = 128 // keys
+        lane_head = lane // keys
+        diagonal = (
+            lax.broadcasted_iota(jnp.int32, (wide, group), 0) // keys
+            == lax.broadcasted_iota(jnp.int32, (wide, group), 1) // HEAD_DIM
+        )
+        collect = (
+            lax.broadcasted_iota(jnp.int32, (cols, 128), 0) // keys
+            == lax.broadcasted_iota(jnp.int32, (cols, 128), 1)
+        ).astype(jnp.bfloat16)
+
         def widened(c, g, base):
             part = jnp.concatenate(
                 [
-                    kv[g, position_ref[(chunk * chunk_spans + c) * neighbors + n]][
+                    source[g, position_ref[(chunk * chunk_spans + c) * neighbors + n]][
                         :, base : base + group
                     ]
                     for n in range(neighbors)
+                    for source in sources
                 ],
                 axis=0,
             )
@@ -382,7 +545,7 @@
             rows = slice(c * SPAN_LEN, (c + 1) * SPAN_LEN)
             for g in range(head_size):
                 score[rows, g * wide : (g + 1) * wide] = lax.dot_general(
-                    queries[g, chunk * chunk_spans + c],
+                    queries[g, order_ref[chunk * chunk_spans + c]],
                     widened(c, g, 0),
                     (((1,), (1,)), ((), ())),
                     preferred_element_type=jnp.float32,
@@ -393,15 +556,19 @@
             top_all = jnp.zeros((SPAN_LEN, 128), jnp.float32)
             for t in range(heads // pair):
                 s = score[rows, t * 128 : (t + 1) * 128]
-                peak = None
-                for n in range(pair):
-                    m = jnp.max(jnp.where(lane_head == n, s, -jnp.inf), axis=1, keepdims=True)
-                    peak = m if peak is None else jnp.where(lane_head == n, m, peak)
-                    top_all = jnp.where(lane == t * pair + n, m, top_all)
+                if pair == 1:
+                    peak = jnp.max(s, axis=1, keepdims=True)
+                    top_all = jnp.where(lane == t, peak, top_all)
+                else:
+                    peak = None
+                    for n in range(pair):
+                        m = jnp.max(jnp.where(lane_head == n, s, -jnp.inf), axis=1, keepdims=True)
+                        peak = m if peak is None else jnp.where(lane_head == n, m, peak)
+                        top_all = jnp.where(lane == t * pair + n, m, top_all)
                 expo[rows, t * 128 : (t + 1) * 128] = jnp.exp(s - peak).astype(jnp.bfloat16)
             tops.append(top_all)
         top_all = jnp.concatenate(tops, axis=0)
-        total = jnp.dot(expo[...], collect, preferred_element_type=jnp.float32)
+        total = jnp.dot(expo[:, :cols], collect, preferred_element_type=jnp.float32)
         top_rows = top_all.T[:heads]
         top[chunk % 2] = top_rows
         lse[plane, chunk] = top_rows + jnp.log(total.T[:heads])
@@ -414,6 +581,26 @@
                     preferred_element_type=jnp.float32,
                 ).astype(ctx.dtype)
 
+    def lse_across(chunk):
+        return pltpu.make_async_remote_copy(
+            src_ref=lse.at[plane, chunk],
+            dst_ref=lse.at[plane, chunk],
+            send_sem=lse_send.at[chunk, 0],
+            recv_sem=lse_recv.at[chunk, 0],
+            device_id=(me, last - plane),
+            device_id_type=LINK,
+        )
+
+    def lse_across_landed(chunk):
+        return pltpu.make_async_remote_copy(
+            src_ref=lse.at[last - plane, chunk],
+            dst_ref=lse.at[last - plane, chunk],
+            send_sem=lse_send.at[chunk, 0],
+            recv_sem=lse_recv.at[chunk, 0],
+            device_id=(me, last - plane),
+            device_id_type=LINK,
+        )
+
     def lse_copy(chunk, k):
         return pltpu.make_async_remote_copy(
             src_ref=lse.at[plane, chunk],
@@ -435,8 +622,8 @@
             device_id_type=LINK,
         )
 
-    def project(chunk):
-        every = lse[:, chunk]
+    def project(chunk, first, end):
+        every = lse[first:end, chunk]
         highest = jnp.max(every, axis=0)
         total = jnp.sum(jnp.exp(every - highest[None]), axis=0)
         scale = jnp.exp(top[chunk % 2] - highest) / total
@@ -460,8 +647,8 @@
 
     def right_copy(chunk, q, to):
         return pltpu.make_async_remote_copy(
-            src_ref=right.at[chunk, q],
-            dst_ref=right.at[chunk, q],
+            src_ref=right.at[chunk, q - 1],
+            dst_ref=right.at[chunk, q - 1],
             send_sem=right_send.at[chunk, q],
             recv_sem=right_recv.at[chunk, q],
             device_id=(me, to),
@@ -479,85 +666,137 @@
         )
 
     def step(it, carry):
-        @pl.when(it < chunks)
-        def _():
-            attend(it)
+        @pl.when((it < chunks) & ~is_b(it))
+        def _():
+            attend(it, (kv_a,))
             for k in range(1, head_size):
                 lse_copy(it, k).start()
 
-        @pl.when((it >= 1) & (it <= chunks))
+        if split:
+
+            @pl.when((it == 2) & middle)
+            def _():
+                relayed(far, chips)
+                keys_c(far, chips)
+
+            @pl.when((it < chunks) & is_b(it) & middle)
+            def _():
+                attend(it, (kv_b, kv_c))
+                lse_across(it).start()
+
+        before = it - 1
+
+        @pl.when((before >= 0) & (before < chunks) & ~is_b(before))
         def _():
             for k in range(1, head_size):
-                lse_landed(it - 1, k).wait_recv()
-            project(it - 1)
+                lse_landed(before, k).wait_recv()
+            project(before, 0, head_size)
+
+        if split:
+
+            @pl.when((before >= 0) & (before < chunks) & is_b(before) & middle)
+            def _():
+                lse_across_landed(before).wait_recv()
+                project(before, 1, last)
 
         to_right = it - 1 - plane
-        right_on = (to_right >= 0) & (to_right < chunks)
+        right_b = is_b(to_right)
+        right_on = (to_right >= 0) & (to_right < chunks) & (~right_b | middle)
+        right_first = (plane == 0) | (right_b & (plane == 1))
         to_left = it - 1 - (last - plane)
-        left_on = (to_left >= 0) & (to_left < chunks)
+        left_b = is_b(to_left)
+        left_on = (to_left >= 0) & (to_left < chunks) & (~left_b | middle)
+        left_first = (plane == last) | (left_b & (plane == last - 1))
         for q in range(head_size):
-
-            @pl.when(right_on & (q > plane) & (plane == 0))
-            def _():
-                right[to_right, q] = own[to_right % head_size, q].astype(right.dtype)
-
-            @pl.when(right_on & (q > plane) & (plane > 0))
-            def _():
-                right_copy(to_right, q, plane).wait_recv()
-                right[to_right, q] = (
-                    own[to_right % head_size, q] + right[to_right, q].astype(jnp.float32)
-                ).astype(right.dtype)
-
-            @pl.when(left_on & (q < plane) & (plane == last))
-            def _():
-                left[to_left, q] = own[to_left % head_size, q].astype(left.dtype)
-
-            @pl.when(left_on & (q < plane) & (plane < last))
-            def _():
-                left_copy(to_left, q, plane).wait_recv()
-                left[to_left, q] = (
-                    own[to_left % head_size, q] + left[to_left, q].astype(jnp.float32)
-                ).astype(left.dtype)
+            if q > 0:
+
+                @pl.when(right_on & (q > plane) & right_first)
+                def _():
+                    right[to_right, q - 1] = own[to_right % head_size, q].astype(right.dtype)
+
+                @pl.when(right_on & (q > plane) & ~right_first)
+                def _():
+                    right_copy(to_right, q, plane).wait_recv()
+                    right[to_right, q - 1] = (
+                        own[to_right % head_size, q] + right[to_right, q - 1].astype(jnp.float32)
+                    ).astype(right.dtype)
+
+            if q < last:
+
+                @pl.when(left_on & (q < plane) & left_first)
+                def _():
+                    left[to_left, q] = own[to_left % head_size, q].astype(left.dtype)
+
+                @pl.when(left_on & (q < plane) & ~left_first)
+                def _():
+                    left_copy(to_left, q, plane).wait_recv()
+                    left[to_left, q] = (
+                        own[to_left % head_size, q] + left[to_left, q].astype(jnp.float32)
+                    ).astype(left.dtype)
 
         for q in range(head_size):
-
-            @pl.when(right_on & (q > plane))
-            def _():
-                right_copy(to_right, q, plane + 1).start()
-
-            @pl.when(left_on & (q < plane))
-            def _():
-                left_copy(to_left, q, plane - 1).start()
+            if q > 0:
+
+                @pl.when(right_on & (q > plane))
+                def _():
+                    right_copy(to_right, q, plane + 1).start()
+
+            if q < last:
+
+                @pl.when(left_on & (q < plane))
+                def _():
+                    left_copy(to_left, q, plane - 1).start()
 
         done = it - 1 - jnp.maximum(plane, last - plane)
-
-        @pl.when((done >= 0) & (done < chunks))
-        def _():
-            @pl.when(plane == 0)
+        done_b = is_b(done)
+        done_on = (done >= 0) & (done < chunks)
+        has_own = ~done_b | middle
+        has_right = (plane > 1) | ((plane == 1) & ~done_b)
+        has_left = (plane < last - 1) | ((plane == last - 1) & ~done_b)
+
+        @pl.when(done_on)
+        def _():
+            @pl.when(has_left)
             def _():
                 left_copy(done, plane, plane).wait_recv()
-                put(done, own[done % head_size, plane] + left[done, plane].astype(jnp.float32))
-
-            @pl.when(plane == last)
+
+            @pl.when(has_right)
             def _():
                 right_copy(done, plane, plane).wait_recv()
-                put(done, own[done % head_size, plane] + right[done, plane].astype(jnp.float32))
-
-            @pl.when((plane > 0) & (plane < last))
-            def _():
-                left_copy(done, plane, plane).wait_recv()
-                right_copy(done, plane, plane).wait_recv()
-                put(
-                    done,
-                    own[done % head_size, plane]
-                    + left[done, plane].astype(jnp.float32)
-                    + right[done, plane].astype(jnp.float32),
-                )
+
+            def from_left_buffer():
+                return left[done, jnp.minimum(plane, last - 1)].astype(jnp.float32)
+
+            def from_right_buffer():
+                return right[done, jnp.maximum(plane - 1, 0)].astype(jnp.float32)
+
+            def mine():
+                return own[done % head_size, plane]
+
+            @pl.when(has_own & has_left & has_right)
+            def _():
+                put(done, mine() + from_left_buffer() + from_right_buffer())
+
+            @pl.when(has_own & has_left & ~has_right)
+            def _():
+                put(done, mine() + from_left_buffer())
+
+            @pl.when(has_own & ~has_left & has_right)
+            def _():
+                put(done, mine() + from_right_buffer())
+
+            @pl.when(~has_own & has_left)
+            def _():
+                put(done, from_left_buffer())
+
+            @pl.when(~has_own & has_right)
+            def _():
+                put(done, from_right_buffer())
 
         return carry
 
     def put(chunk, value):
-        final[pl.ds(chunk * chunk_spans, chunk_spans)] = value.reshape(
+        final[pl.ds(chunk * chunk_spans, chunk_spans)] = value.astype(final.dtype).reshape(
             chunk_spans, SPAN_LEN, group
         )
 
@@ -566,9 +805,11 @@
     out_row = lax.broadcasted_iota(jnp.int32, (SPAN_LEN, group), 0)
 
     def move_down(b, carry):
-        before = jnp.where(b % blocks_seq != 0, final[(b + blocks - 1) % blocks], 0.0)
+        previous = final[place_ref[(b + blocks - 1) % blocks]].astype(jnp.float32)
+        before = jnp.where(b % blocks_seq != 0, previous, 0.0)
+        here = final[place_ref[b]].astype(jnp.float32)
         moved = jnp.where(
-            out_row == SPAN_LEN - 1, final[b][0:1], pltpu.roll(before, SPAN_LEN - 1, 0)
+            out_row == SPAN_LEN - 1, here[0:1], pltpu.roll(before, SPAN_LEN - 1, 0)
         )
         o_ref[b] = moved.astype(o_ref.dtype)
         return carry
@@ -577,7 +818,9 @@
 
     for k in range(1, span_size):
         ask(k).wait_send()
-        enc_copy(k).wait_send()
+        enc_copy(k, 0).wait_send()
+        if split:
+            enc_copy(k, 1).wait_send()
     for which in range(2):
 
         @pl.when(plane < last)
@@ -592,32 +835,72 @@
 
             @pl.when(plane - k >= 0)
             def _():
-                @pl.when(plane < last)
+                shard = plane - k
+
+                @pl.when((plane < last) & whole_hop(which, shard, plane + 1))
                 def _():
-                    line_copy(which, plane - k, plane + 1, 0).wait_send()
-
-                pair_copy(which, plane - k).wait_send()
+                    line_copy(which, shard, plane + 1, 0).wait_send()
+
+                @pl.when((plane < last) & ~whole_hop(which, shard, plane + 1))
+                def _():
+                    for copy in end_pieces(shard, plane + 1):
+                        copy.wait_send()
+
+                pair_copy(which, shard).wait_send()
 
             @pl.when(plane + k <= last)
             def _():
-                @pl.when(plane > 0)
+                shard = plane + k
+
+                @pl.when((plane > 0) & whole_hop(which, shard, plane - 1))
                 def _():
-                    line_copy(which, plane + k, plane - 1, 1).wait_send()
-
-                pair_copy(which, plane + k).wait_send()
+                    line_copy(which, shard, plane - 1, 1).wait_send()
+
+                @pl.when((plane > 0) & ~whole_hop(which, shard, plane - 1))
+                def _():
+                    for copy in end_pieces(shard, plane - 1):
+                        copy.wait_send()
+
+                pair_copy(which, shard).wait_send()
+
+    def far_sent(shard):
+        for copy in shared_pieces(shard):
+            copy.wait_send()
+
+    far_shard(far_sent)
+    if split:
+
+        @pl.when(~middle)
+        def _():
+            for k in range(span_size):
+                relay_copy(k).wait_send()
+
 
     def drain(chunk, carry):
-        for k in range(1, head_size):
-            lse_copy(chunk, k).wait_send()
+        @pl.when(~is_b(chunk))
+        def _():
+            for k in range(1, head_size):
+                lse_copy(chunk, k).wait_send()
+
+        if split:
+
+            @pl.when(is_b(chunk) & middle)
+            def _():
+                lse_across(chunk).wait_send()
+
+        on = ~is_b(chunk) | middle
         for q in range(head_size):
-
-            @pl.when(q > plane)
-            def _():
-                right_copy(chunk, q, plane + 1).wait_send()
-
-            @pl.when(q < plane)
-            def _():
-                left_copy(chunk, q, plane - 1).wait_send()
+            if q > 0:
+
+                @pl.when(on & (q > plane))
+                def _():
+                    right_copy(chunk, q, plane + 1).wait_send()
+
+            if q < last:
+
+                @pl.when(on & (q < plane))
+                def _():
+                    left_copy(chunk, q, plane - 1).wait_send()
 
         return carry
 
@@ -625,7 +908,17 @@
 
 
 def fused(
-    position, request, states, encodings, query_weight, key_weight, value_weight, out_weight
+    rows_a,
+    position,
+    order,
+    place,
+    request,
+    states,
+    encodings,
+    query_weight,
+    key_weight,
+    value_weight,
+    out_weight,
 ):
     span_size = lax.axis_size("span")
     head_size = lax.axis_size("head")
@@ -634,47 +927,58 @@
     group = query_weight.shape[1]
     entries = position.shape[0]
     per_peer = entries // span_size
+    rows_b = per_peer - rows_a
+    held_b = max(rows_b, 1)
     blocks = rows // SPAN_LEN
     chunks = blocks // CHUNK_SPANS
     chunk_rows = CHUNK_SPANS * SPAN_LEN
     heads = head_size * group // HEAD_DIM
-    score_cols = heads * (entries // blocks) * tokens
+    score_cols = heads * (entries // blocks) * tokens * (2 if rows_b else 1)
     bf16, f32 = jnp.bfloat16, jnp.float32
     dma = pltpu.SemaphoreType.DMA
     vmem = pl.BlockSpec(memory_space=pltpu.VMEM)
+    smem = pl.BlockSpec(memory_space=pltpu.SMEM)
     hbm = pl.BlockSpec(memory_space=pl.ANY)
     return pl.pallas_call(
-        functools.partial(kernel, span_size, head_size),
+        functools.partial(kernel, span_size, head_size, rows_a),
         out_shape=jax.ShapeDtypeStruct((blocks, SPAN_LEN, group), bf16),
-        in_specs=[pl.BlockSpec(memory_space=pltpu.SMEM), vmem] + [hbm] * 6,
+        in_specs=[smem] * 3 + [vmem] + [hbm] * 6,
         out_specs=vmem,
         scratch_shapes=[
             pltpu.VMEM((slots, tokens, model), bf16),
             pltpu.VMEM((span_size, per_peer, tokens, model), bf16),
-            pltpu.VMEM((span_size, per_peer, tokens, model), bf16),
+            pltpu.VMEM((span_size, rows_a, tokens, model), bf16),
+            pltpu.VMEM((span_size if rows_b else 1, held_b, tokens, model), bf16),
+            pltpu.VMEM((span_size if rows_b else 1, held_b, tokens, model), bf16),
             pltpu.VMEM((head_size, model, 3 * group), bf16),
             pltpu.VMEM((head_size, group, model), bf16),
             pltpu.VMEM((blocks, SPAN_LEN, model), bf16),
             pltpu.VMEM((head_size, blocks, SPAN_LEN, group), bf16),
-            pltpu.VMEM((head_size, entries, tokens, 2 * group), bf16),
+            pltpu.VMEM((head_size, span_size * rows_a, tokens, 2 * group), bf16),
+            pltpu.VMEM((head_size, max(span_size * rows_b, 1), tokens, 2 * group), bf16),
+            pltpu.VMEM((head_size, max(span_size * rows_b, 1), tokens, 2 * group), bf16),
             pltpu.VMEM((head_size, head_size, chunk_rows, group), f32),
-            pltpu.VMEM((chunks, head_size, chunk_rows, group), bf16),
-            pltpu.VMEM((chunks, head_size, chunk_rows, group), bf16),
+            pltpu.VMEM((chunks, head_size - 1, chunk_rows, group), bf16),
+            pltpu.VMEM((chunks, head_size - 1, chunk_rows, group), bf16),
             pltpu.VMEM((head_size, chunks, heads, chunk_rows), f32),
             pltpu.VMEM((2, heads, chunk_rows), f32),
             pltpu.VMEM((2, chunk_rows, model), bf16),
             pltpu.VMEM((chunk_rows, score_cols), f32),
             pltpu.VMEM((chunk_rows, score_cols), bf16),
-            pltpu.VMEM((blocks, SPAN_LEN, group), f32),
+            pltpu.VMEM((blocks, SPAN_LEN, group), bf16),
             pltpu.VMEM(request.shape, jnp.int32),
             pltpu.SMEM(request.shape, jnp.int32),
             dma((7,)),
             dma((span_size,)),
             dma((span_size,)),
+            dma((2, span_size)),
+            dma((2, span_size)),
             dma((span_size,)),
             dma((span_size,)),
             dma((2, head_size, 2)),
             dma((2, head_size)),
+            dma((4,)),
+            dma((4,)),
             dma((2, head_size)),
             dma((2, head_size)),
             dma((chunks, head_size)),
@@ -692,6 +996,8 @@
         ),
     )(
         position,
+        order,
+        place,
         request,
         states.reshape(blocks, SPAN_LEN, model),
         encodings,
@@ -702,26 +1008,103 @@
     )
 
 
+def take(values, index):
+    numbering = jnp.arange(values.shape[0], dtype=jnp.int32)
+    return jnp.sum(jnp.where(index[:, None] == numbering[None, :], values[None, :], 0), axis=1)
+
+
+def put_at(values, index):
+    numbering = jnp.arange(values.shape[0], dtype=jnp.int32)
+    return jnp.sum(jnp.where(index[None, :] == numbering[:, None], values[None, :], 0), axis=1)
+
+
+def other_half(values):
+    return values.reshape(-1, 2)[:, ::-1].reshape(-1)
+
+
+def orbit_min(start, step, length):
+    reach = 1
+    while reach < length:
+        start = jnp.minimum(start, take(start, step))
+        reach *= 2
+        if reach < length:
+            step = take(step, step)
+    return start
+
+
+def earlier(same):
+    numbering = jnp.arange(same.shape[0], dtype=jnp.int32)
+    return jnp.sum((same & (numbering[None, :] < numbering[:, None])).astype(jnp.int32), axis=1)
+
+
+def paired(same, rank):
+    numbering = jnp.arange(rank.shape[0], dtype=jnp.int32)
+    beside = rank + 1 - 2 * (rank % 2)
+    return jnp.sum(jnp.where(same & (rank[None, :] == beside[:, None]), numbering[None, :], 0), axis=1)
+
+
+def halve(shard_ids):
+    entries = shard_ids.shape[0]
+    numbering = jnp.arange(entries, dtype=jnp.int32)
+    same = shard_ids[:, None] == shard_ids[None, :]
+    beside = paired(same, earlier(same))
+    low = orbit_min(numbering, beside + 1 - 2 * (beside % 2), entries // 2)
+    enters = low > other_half(low)
+    same = same & (enters[:, None] == enters[None, :])
+    beside = paired(same, earlier(same))
+    follow = beside + 1 - 2 * (beside % 2)
+    low = orbit_min(numbering // 2, take(follow, follow), entries // 4)
+    return (low > take(low, follow)).astype(jnp.int32)
+
+
 def body(
     decoder_states, encodings, neighbor_table, query_weight, key_weight, value_weight, out_weight
 ):
     peer_count = lax.axis_size("span")
+    head_size = lax.axis_size("head")
+    spans, neighbors = neighbor_table.shape[:2]
     shard_ids = neighbor_table[:, :, 0].reshape(-1)
     slot_ids = neighbor_table[:, :, 1].reshape(-1)
     entries = shard_ids.shape[0]
     per_peer = entries // peer_count
-    numbering = jnp.arange(entries, dtype=jnp.int32)
-    same_before = (shard_ids[:, None] == shard_ids[None, :]) & (
-        numbering[None, :] < numbering[:, None]
+    split = (
+        neighbors == 2
+        and per_peer % 4 == 0
+        and head_size == 4
+        and spans % (2 * CHUNK_SPANS) == 0
+        and spans >= 4 * CHUNK_SPANS
     )
-    ranking = jnp.sum(same_before.astype(jnp.int32), axis=1)
-    position = shard_ids * per_peer + ranking
-    placed = position[None, :] == numbering[:, None]
-    request = jnp.sum(jnp.where(placed, slot_ids[None, :], 0), axis=1)
-    request = request.reshape(peer_count, 1, per_peer)
+    rows_a = per_peer // 2 if split else per_peer
+    same = shard_ids[:, None] == shard_ids[None, :]
+    numbering = jnp.arange(spans, dtype=jnp.int32)
+    if split:
+        half = halve(shard_ids)
+        ranking = earlier(same & (half[:, None] == half[None, :]))
+        span_half = half.reshape(-1, 2)[:, 0]
+        span_rank = earlier(span_half[:, None] == span_half[None, :])
+        count = span_rank // CHUNK_SPANS
+        chunks = spans // CHUNK_SPANS
+        chunk = jnp.where(
+            span_half == 0,
+            jnp.maximum(2 * count - 1, 0),
+            jnp.minimum(2 * count + 2, chunks - 1),
+        )
+        place = chunk * CHUNK_SPANS + span_rank % CHUNK_SPANS
+        order = put_at(numbering, place)
+        asked_at = shard_ids * per_peer + half * rows_a + ranking
+        entry_place = (place[:, None] * 2 + jnp.arange(2, dtype=jnp.int32)[None, :]).reshape(-1)
+        position = put_at(shard_ids * rows_a + ranking, entry_place)
+    else:
+        ranking = earlier(same)
+        place = order = numbering
+        asked_at = position = shard_ids * per_peer + ranking
+    request = put_at(slot_ids, asked_at).reshape(peer_count, 1, per_peer)
     request = jnp.pad(request, ((0, 0), (0, 7), (0, 128 - per_peer)))
     out = fused(
+        rows_a,
         position,
+        order,
+        place,
         request,
         decoder_states,
         encodings,

time: 187 us -> 163 us (0.87)
  Pallas kernels: 181 us -> 153 us
  other arithmetic: 0.29 us -> 4.93 us
    pallas_call x1, Pallas kernels: 181 us -> 153 us  [fused(): pl.pallas_call(functools.partial(kernel, span_size, head_size, rows_a), o...]
    reduce_sum x2 -> x19, other arithmetic: 0.29 us -> 4.41 us  [the longest x11 1.96 us: take(): jnp.sum(jnp.where(index[:, None] == numbering[None, :], values[None, :],...]
where the time goes in v2:
time: 163 us
  Pallas kernels  153 us (94%)
  local copies, waits for them, and re-layouts  5.48 us (3%)
  other arithmetic  4.93 us (3%)
    pallas_call x1, Pallas kernels, fused(): pl.pallas_call(functools.partial(kernel, span_size, head_size, rows_a), o...  153 us

profile of v2, /device:TPU:0, one launch (start us, length us, event | category | flops | bytes accessed | tf_op | source)
XLA Modules:
  0.0 163.2 jit_solution(2155168000626921706)
XLA Ops:
  0.0 0.8 fusion.31
  0.8 0.1 copy.27
  0.9 0.1 broadcast_in_dim.245
  1.0 0.1 copy.22
  1.1 0.1 eq.107
  1.2 0.2 convert_reduce_fusion.2
  1.4 0.2 select_reduce_fusion.21
  1.6 0.2 select_reduce_fusion.19
  1.8 0.2 select_reduce_fusion.17
  2.0 0.2 select_reduce_fusion.15
  2.2 0.2 select_reduce_fusion.13
  2.4 0.2 select_reduce_fusion.12
  2.5 0.1 reduce_sum.279
  2.6 0.1 reduce_sum.278
  2.8 0.1 reduce_sum.276
  2.9 0.1 reduce_sum.277
  3.0 0.1 reduce_sum.280
  3.1 0.1 rev.3
  3.2 0.1 reshape.485
  3.3 0.2 convert_reduce_fusion.1
  3.5 0.2 select_reduce_fusion.11
  3.7 0.2 select_reduce_fusion.10
  3.9 0.2 select_reduce_fusion.8
  4.1 0.2 select_reduce_fusion.6
  4.3 0.2 select_reduce_fusion.4
  4.5 0.2 select_reduce_fusion.3
  4.7 0.2 select_reduce_fusion.2
  4.9 0.2 convert_reduce_fusion
  5.1 0.1 reduce_sum.296
  5.2 0.1 reduce_sum.294
  5.3 0.1 reduce_sum.291
  5.4 0.1 reduce_sum.285
  5.5 0.1 reduce_sum.288
  5.6 0.1 convert_reduce_fusion.3
  5.8 0.2 convert_reduce_fusion.4
  6.0 0.0 copy-start
  6.0 0.6 select_reduce_fusion.22.order_ref
  6.6 0.1 copy.23
  6.7 0.1 fusion.6
  6.8 0.1 iota_add_fusion
  6.9 0.1 add.241
  7.0 0.7 select_reduce_fusion
  7.7 0.1 reshape.486
  7.8 0.6 pad.4.request_ref
  8.4 0.0 copy-done
  8.4 152.5 %shard_map.73 = bf16[32,64,256]{2,1,0:T(8,128)(2,1)} custom-call(s32[64]{0:T(128)} %get-tuple-element.26.position_ref, s32[32]{0:T(128)} %select_reduce_fusion.22.order_ref, s32[32]{0:T(128)} %copy-done, s32[8,8,128]{2,1,0:T(8,128)} %pad.4.request_ref, bf16[32,64,1024]{2,1,0:T(8,128)(2,1)} %bitcast.11, bf16[64,32,1024]{2,1,0:T(8,128)(2,1)} %encodings_hbm.1, ...), custom_call_target="tpu_custom_call" | custom-call | flops 12884901888 | bytes 16777216 | tf_op jit(solution)/shard_map/pallas_call | solution.py:942
  160.9 2.3 %copy.30 = bf16[2048,256]{1,0:T(8,128)(2,1)} copy(bf16[2048,256]{1,0:T(8,128)(2,1)} %bitcast.8) | data formatting | bytes 2097152
  (21 shorter events, 0.2 us)
Async XLA Ops:
  6.0 2.5 %copy-start = (s32[32]{0:T(128)}, s32[32]{0:T(128)S(1)}, u32[]{:S(2)}) copy-start(s32[32]{0:T(128)S(1)} %fusion.14.place_ref) | copy-start | bytes 388

commit v3 on v2

--- a/solution.py
+++ b/solution.py
@@ -11,7 +11,8 @@
 SPAN_LEN = 64
 SEQ_LEN = 2048
 VMEM = 63 * 1024 * 1024
-CHUNK_SPANS = 4
+CHUNK_SPANS = 2
+AHEAD = 3
 LINK = pl.DeviceIdType.MESH
 
 
@@ -28,10 +29,7 @@
     span_size,
     head_size,
     rows_a,
-    position_ref,
-    order_ref,
-    place_ref,
-    request_ref,
+    table_ref,
     states_hbm,
     encodings_hbm,
     query_hbm,
@@ -51,15 +49,16 @@
     kv_a,
     kv_b,
     kv_c,
-    own,
+    own_a,
+    own_b,
     right,
     left,
     lse,
     top,
-    ctx,
     score,
     expo,
     final,
+    plan,
     asked,
     asked_s,
     local_sem,
@@ -86,6 +85,7 @@
     plane = lax.axis_index("head")
     core = me % 2
     last = head_size - 1
+    blocks = states.shape[0]
     partner = me + 1 - 2 * core
     slots, tokens, model = encodings_hbm.shape
     per_peer = sent.shape[1]
@@ -104,7 +104,6 @@
     ]
     for copy in own_copies:
         copy.start()
-    asked[me] = request_ref[me]
 
     barrier = pltpu.get_barrier_semaphore()
     for k in range(1, span_size):
@@ -120,7 +119,7 @@
     def ask(k):
         peer = flip(me, k, span_size)
         return pltpu.make_async_remote_copy(
-            src_ref=request_ref.at[peer],
+            src_ref=plan,
             dst_ref=asked.at[me],
             send_sem=ask_send.at[k],
             recv_sem=ask_recv.at[k],
@@ -131,7 +130,7 @@
     def landed(k):
         peer = flip(me, k, span_size)
         return pltpu.make_async_remote_copy(
-            src_ref=request_ref.at[peer],
+            src_ref=plan,
             dst_ref=asked.at[peer],
             send_sem=ask_send.at[k],
             recv_sem=ask_recv.at[k],
@@ -139,8 +138,6 @@
             device_id_type=LINK,
         )
 
-    for k in range(1, span_size):
-        ask(k).start()
 
     halves = ((weights, weights.shape[1] // 2, 0), (outs, outs.shape[1] // 2, 1))
 
@@ -284,6 +281,23 @@
     def _():
         send_own(1)
 
+
+    entries = table_ref.shape[1]
+    request, position, order, place = plan_rows(
+        table_ref[0:1, :], table_ref[1:2, :], per_peer, rows_a, entries // blocks
+    )
+    plan[...] = jnp.zeros_like(plan)
+    asked[me] = jnp.zeros(plan.shape, plan.dtype)
+    plan[0:1, 0:entries] = request
+    plan[1:2, 0:entries] = position
+    plan[2:3, 0:entries] = order
+    plan[3:4, 0:entries] = place
+    asked[me, 0:1, 0:entries] = request
+    asked[me, 1:2, 0:entries] = position
+    asked[me, 2:3, 0:entries] = order
+    asked[me, 3:4, 0:entries] = place
+    for k in range(1, span_size):
+        ask(k).start()
 
     for k in range(1, span_size):
         landed(k).wait_recv()
@@ -334,7 +348,7 @@
 
     def pick(buf, peer, offset, begin, count):
         for j in range(count):
-            buf[peer, offset + j] = enc[asked_s[peer, 0, begin + j]]
+            buf[peer, offset + j] = enc[asked_s[peer, 0, me * per_peer + begin + j]]
 
     def pick_and_send(part, begin, count):
         def one(k, carry):
@@ -355,7 +369,7 @@
     pick_and_send(0, 0, rows_a)
 
     own_copies[4].wait()
-    blocks, block_len, _ = states.shape
+    block_len = states.shape[1]
     blocks_seq = SEQ_LEN // block_len
     row = lax.broadcasted_iota(jnp.int32, (block_len, model), 0)
 
@@ -371,7 +385,7 @@
     lax.fori_loop(0, blocks, move_up, 0)
 
     def project_queries(shard):
-        step = min(4, blocks)
+        step = min(16, blocks)
 
         def one(b, carry):
             x = states[pl.ds(b * step, step)].reshape(step * block_len, model)
@@ -399,6 +413,20 @@
 
         lax.fori_loop(first, end, one, 0)
 
+    def project_all_keys(shard, src, dst):
+        count = src.shape[1]
+        step = min(4, span_size)
+
+        def one(i, carry):
+            x = src[pl.ds(i * step, step)].reshape(step * count * tokens, model)
+            y = jnp.dot(x, weights[shard, :, 0 : 2 * group], preferred_element_type=jnp.float32)
+            dst[shard, pl.ds(i * step * count, step * count)] = y.astype(dst.dtype).reshape(
+                step * count, tokens, 2 * group
+            )
+            return carry
+
+        lax.fori_loop(0, span_size // step, one, 0)
+
     def shards_at(k, work):
         if k == 0:
             work(plane)
@@ -418,8 +446,8 @@
     def keys_a(k, first, end):
         shards_at(k, lambda shard: project_keys(shard, arrived_a, kv_a, first, end))
 
-    def keys_b(k, first, end):
-        shards_at(k, lambda shard: project_keys(shard, arrived_b, kv_b, first, end))
+    def keys_b(k):
+        shards_at(k, lambda shard: project_all_keys(shard, arrived_b, kv_b))
 
     def keys_c(first, end):
         for shard in range(head_size):
@@ -469,7 +497,7 @@
         def _():
             wait_enc(1, 0, chips)
             for k in range(last):
-                keys_b(k, 0, chips)
+                keys_b(k)
 
     wait_enc(0, near, far)
     for k in range(last):
@@ -485,33 +513,17 @@
     far_shard(far_shared)
     wait_pair(0, last)
     shards_at(last, project_queries)
-    keys_a(last, 0, chips)
-    @pl.when(~middle)
-    def _():
-        for k in range(1, last):
-            pass_on(1, k)
-
-    pass_on(1, last)
-    for k in range(1, head_size):
-        wait_pair(1, k)
-    if split:
-        @pl.when(middle)
-        def _():
-            relayed(0, far)
-            keys_c(0, far)
-
+    shards_at(last, lambda shard: project_all_keys(shard, arrived_a, kv_a))
 
     chunks = blocks // CHUNK_SPANS
     chunk_spans = CHUNK_SPANS
     heads = head_size * group // HEAD_DIM
-    neighbors = position_ref.shape[0] // blocks
+    neighbors = entries // blocks
     packed = group // HEAD_DIM
     lane = lax.broadcasted_iota(jnp.int32, (SPAN_LEN, 128), 1)
 
-    def is_b(chunk):
-        if not split:
-            return chunk < 0
-        return ((chunk >= 2) & (chunk % 2 == 0)) | (chunk == chunks - 1)
+    chunks_b = chunks // 2 if split else 0
+    chunks_a = chunks - chunks_b
 
     def attend(chunk, sources):
         keys = neighbors * len(sources) * tokens
@@ -531,7 +543,7 @@
         def widened(c, g, base):
             part = jnp.concatenate(
                 [
-                    source[g, position_ref[(chunk * chunk_spans + c) * neighbors + n]][
+                    source[g, asked_s[me, 1, (chunk * chunk_spans + c) * neighbors + n]][
                         :, base : base + group
                     ]
                     for n in range(neighbors)
@@ -545,7 +557,7 @@
             rows = slice(c * SPAN_LEN, (c + 1) * SPAN_LEN)
             for g in range(head_size):
                 score[rows, g * wide : (g + 1) * wide] = lax.dot_general(
-                    queries[g, order_ref[chunk * chunk_spans + c]],
+                    queries[g, asked_s[me, 2, (chunk * chunk_spans + c) * neighbors]],
                     widened(c, g, 0),
                     (((1,), (1,)), ((), ())),
                     preferred_element_type=jnp.float32,
@@ -570,16 +582,16 @@
         top_all = jnp.concatenate(tops, axis=0)
         total = jnp.dot(expo[:, :cols], collect, preferred_element_type=jnp.float32)
         top_rows = top_all.T[:heads]
-        top[chunk % 2] = top_rows
+        top[chunk] = top_rows
         lse[plane, chunk] = top_rows + jnp.log(total.T[:heads])
         for c in range(chunk_spans):
             rows = slice(c * SPAN_LEN, (c + 1) * SPAN_LEN)
             for g in range(head_size):
-                ctx[chunk % 2, rows, g * group : (g + 1) * group] = jnp.dot(
+                states[chunk * chunk_spans + c, :, g * group : (g + 1) * group] = jnp.dot(
                     expo[rows, g * wide : (g + 1) * wide],
                     widened(c, g, group),
                     preferred_element_type=jnp.float32,
-                ).astype(ctx.dtype)
+                ).astype(states.dtype)
 
     def lse_across(chunk):
         return pltpu.make_async_remote_copy(
@@ -622,11 +634,11 @@
             device_id_type=LINK,
         )
 
-    def project(chunk, first, end):
+    def project(chunk, first, end, own, slot):
         every = lse[first:end, chunk]
         highest = jnp.max(every, axis=0)
         total = jnp.sum(jnp.exp(every - highest[None]), axis=0)
-        scale = jnp.exp(top[chunk % 2] - highest) / total
+        scale = jnp.exp(top[chunk] - highest) / total
         high = scale.astype(jnp.bfloat16)
         low = (scale - high.astype(jnp.float32)).astype(jnp.bfloat16)
         spread = (
@@ -639,11 +651,12 @@
             (((0,), (0,)), ((), ())),
             preferred_element_type=jnp.float32,
         )
-        scaled = (ctx[chunk % 2].astype(jnp.float32) * factor).astype(jnp.bfloat16)
+        context = states[pl.ds(chunk * chunk_spans, chunk_spans)].reshape(factor.shape)
+        scaled = (context.astype(jnp.float32) * factor).astype(jnp.bfloat16)
         w = outs[...].reshape(head_size * group, model)
         y = jnp.dot(scaled, w, preferred_element_type=jnp.float32)
         for q in range(head_size):
-            own[chunk % head_size, q] = y[:, q * group : (q + 1) * group]
+            own[slot, q] = y[:, q * group : (q + 1) * group]
 
     def right_copy(chunk, q, to):
         return pltpu.make_async_remote_copy(
@@ -665,134 +678,174 @@
             device_id_type=LINK,
         )
 
-    def step(it, carry):
-        @pl.when((it < chunks) & ~is_b(it))
-        def _():
-            attend(it, (kv_a,))
-            for k in range(1, head_size):
-                lse_copy(it, k).start()
-
-        if split:
-
-            @pl.when((it == 2) & middle)
-            def _():
-                relayed(far, chips)
-                keys_c(far, chips)
-
-            @pl.when((it < chunks) & is_b(it) & middle)
-            def _():
-                attend(it, (kv_b, kv_c))
-                lse_across(it).start()
-
-        before = it - 1
-
-        @pl.when((before >= 0) & (before < chunks) & ~is_b(before))
-        def _():
-            for k in range(1, head_size):
-                lse_landed(before, k).wait_recv()
-            project(before, 0, head_size)
-
-        if split:
-
-            @pl.when((before >= 0) & (before < chunks) & is_b(before) & middle)
-            def _():
-                lse_across_landed(before).wait_recv()
-                project(before, 1, last)
-
-        to_right = it - 1 - plane
-        right_b = is_b(to_right)
-        right_on = (to_right >= 0) & (to_right < chunks) & (~right_b | middle)
-        right_first = (plane == 0) | (right_b & (plane == 1))
-        to_left = it - 1 - (last - plane)
-        left_b = is_b(to_left)
-        left_on = (to_left >= 0) & (to_left < chunks) & (~left_b | middle)
-        left_first = (plane == last) | (left_b & (plane == last - 1))
+    def combine(buf, copy, on, first, chunk, q, index, own, slot):
+        @pl.when(on & first)
+        def _():
+            buf[chunk, index] = own[slot, q].astype(buf.dtype)
+
+        @pl.when(on & ~first)
+        def _():
+            copy(chunk, q, plane).wait_recv()
+            buf[chunk, index] = (own[slot, q] + buf[chunk, index].astype(jnp.float32)).astype(
+                buf.dtype
+            )
+
+    def sums(base, to_right, right_on, right_first, to_left, left_on, left_first, own):
+        depth = own.shape[0]
         for q in range(head_size):
             if q > 0:
-
-                @pl.when(right_on & (q > plane) & right_first)
-                def _():
-                    right[to_right, q - 1] = own[to_right % head_size, q].astype(right.dtype)
-
-                @pl.when(right_on & (q > plane) & ~right_first)
-                def _():
-                    right_copy(to_right, q, plane).wait_recv()
-                    right[to_right, q - 1] = (
-                        own[to_right % head_size, q] + right[to_right, q - 1].astype(jnp.float32)
-                    ).astype(right.dtype)
-
+                combine(
+                    right,
+                    right_copy,
+                    right_on & (q > plane),
+                    right_first,
+                    base + to_right,
+                    q,
+                    q - 1,
+                    own,
+                    to_right % depth,
+                )
             if q < last:
-
-                @pl.when(left_on & (q < plane) & left_first)
-                def _():
-                    left[to_left, q] = own[to_left % head_size, q].astype(left.dtype)
-
-                @pl.when(left_on & (q < plane) & ~left_first)
-                def _():
-                    left_copy(to_left, q, plane).wait_recv()
-                    left[to_left, q] = (
-                        own[to_left % head_size, q] + left[to_left, q].astype(jnp.float32)
-                    ).astype(left.dtype)
-
+                combine(
+                    left,
+                    left_copy,
+                    left_on & (q < plane),
+                    left_first,
+                    base + to_left,
+                    q,
+                    q,
+                    own,
+                    to_left % depth,
+                )
         for q in range(head_size):
             if q > 0:
 
                 @pl.when(right_on & (q > plane))
                 def _():
-                    right_copy(to_right, q, plane + 1).start()
+                    right_copy(base + to_right, q, plane + 1).start()
 
             if q < last:
 
                 @pl.when(left_on & (q < plane))
                 def _():
-                    left_copy(to_left, q, plane - 1).start()
-
-        done = it - 1 - jnp.maximum(plane, last - plane)
-        done_b = is_b(done)
-        done_on = (done >= 0) & (done < chunks)
-        has_own = ~done_b | middle
-        has_right = (plane > 1) | ((plane == 1) & ~done_b)
-        has_left = (plane < last - 1) | ((plane == last - 1) & ~done_b)
-
-        @pl.when(done_on)
+                    left_copy(base + to_left, q, plane - 1).start()
+
+    def finish(chunk, on, has_left, has_right, own, slot):
+        @pl.when(on)
         def _():
             @pl.when(has_left)
             def _():
-                left_copy(done, plane, plane).wait_recv()
+                left_copy(chunk, plane, plane).wait_recv()
 
             @pl.when(has_right)
             def _():
-                right_copy(done, plane, plane).wait_recv()
-
-            def from_left_buffer():
-                return left[done, jnp.minimum(plane, last - 1)].astype(jnp.float32)
-
-            def from_right_buffer():
-                return right[done, jnp.maximum(plane - 1, 0)].astype(jnp.float32)
-
-            def mine():
-                return own[done % head_size, plane]
-
-            @pl.when(has_own & has_left & has_right)
-            def _():
-                put(done, mine() + from_left_buffer() + from_right_buffer())
-
-            @pl.when(has_own & has_left & ~has_right)
-            def _():
-                put(done, mine() + from_left_buffer())
-
-            @pl.when(has_own & ~has_left & has_right)
-            def _():
-                put(done, mine() + from_right_buffer())
-
-            @pl.when(~has_own & has_left)
-            def _():
-                put(done, from_left_buffer())
-
-            @pl.when(~has_own & has_right)
-            def _():
-                put(done, from_right_buffer())
-
+                right_copy(chunk, plane, plane).wait_recv()
+
+            def left_sum():
+                return left[chunk, jnp.minimum(plane, last - 1)].astype(jnp.float32)
+
+            def right_sum():
+                return right[chunk, jnp.maximum(plane - 1, 0)].astype(jnp.float32)
+
+            mine = 0.0 if own is None else own[slot, plane]
+
+            @pl.when(has_left & has_right)
+            def _():
+                put(chunk, mine + left_sum() + right_sum())
+
+            @pl.when(has_left & ~has_right)
+            def _():
+                put(chunk, mine + left_sum())
+
+            @pl.when(~has_left & has_right)
+            def _():
+                put(chunk, mine + right_sum())
+
+    def attend_b(index):
+        attend(chunks_a + index, (kv_b, kv_c))
+        lse_across(chunks_a + index).start()
+
+    def attend_a(chunk, carry):
+        attend(chunk, (kv_a,))
+        for k in range(1, head_size):
+            lse_copy(chunk, k).start()
+        return carry
+
+    lax.fori_loop(0, min(AHEAD, chunks_a), attend_a, 0)
+    @pl.when(~middle)
+    def _():
+        for k in range(1, last):
+            pass_on(1, k)
+
+    pass_on(1, last)
+    for k in range(1, head_size):
+        wait_pair(1, k)
+    if split:
+
+        @pl.when(middle)
+        def _():
+            relayed(0, far)
+            keys_c(0, far)
+            relayed(far, chips)
+            keys_c(far, chips)
+            attend_b(0)
+
+    def step(it, carry):
+        @pl.when(it < chunks_a)
+        def _():
+            for k in range(1, head_size):
+                lse_landed(it, k).wait_recv()
+            project(it, 0, head_size, own_a, it % head_size)
+
+        to_right, to_left = it - plane, it - (last - plane)
+        sums(
+            0,
+            to_right,
+            (to_right >= 0) & (to_right < chunks_a),
+            plane == 0,
+            to_left,
+            (to_left >= 0) & (to_left < chunks_a),
+            plane == last,
+            own_a,
+        )
+        if split:
+
+            @pl.when((it < chunks_b) & middle)
+            def _():
+                lse_across_landed(chunks_a + it).wait_recv()
+                project(chunks_a + it, 1, last, own_b, it % own_b.shape[0])
+
+            right_b, left_b = it - (plane - 1), it - (last - 1 - plane)
+            sums(
+                chunks_a,
+                right_b,
+                (right_b >= 0) & (right_b < chunks_b) & middle,
+                plane == 1,
+                left_b,
+                (left_b >= 0) & (left_b < chunks_b) & middle,
+                plane == last - 1,
+                own_b,
+            )
+
+            @pl.when((it + 1 < chunks_b) & middle)
+            def _():
+                attend_b(it + 1)
+
+        @pl.when(it + AHEAD < chunks_a)
+        def _():
+            attend_a(it + AHEAD, 0)
+
+        done = it - jnp.maximum(plane, last - plane)
+        done_on = (done >= 0) & (done < chunks_a)
+        finish(done, done_on, plane < last, plane > 0, own_a, done % head_size)
+        if split:
+            done = it - jnp.maximum(plane - 1, last - 1 - plane)
+            done_on = (done >= 0) & (done < chunks_b)
+            slot = done % own_b.shape[0]
+            finish(
+                chunks_a + done, done_on & middle, plane < last - 1, plane > 1, own_b, slot
+            )
+            finish(chunks_a + done, done_on & ~middle, plane == 0, plane == last, None, 0)
         return carry
 
     def put(chunk, value):
@@ -800,14 +853,14 @@
             chunk_spans, SPAN_LEN, group
         )
 
-    lax.fori_loop(0, chunks + head_size, step, 0)
+    lax.fori_loop(0, chunks_a + last, step, 0)
 
     out_row = lax.broadcasted_iota(jnp.int32, (SPAN_LEN, group), 0)
 
     def move_down(b, carry):
-        previous = final[place_ref[(b + blocks - 1) % blocks]].astype(jnp.float32)
+        previous = final[asked_s[me, 3, (b + blocks - 1) % blocks * neighbors]].astype(jnp.float32)
         before = jnp.where(b % blocks_seq != 0, previous, 0.0)
-        here = final[place_ref[b]].astype(jnp.float32)
+        here = final[asked_s[me, 3, b * neighbors]].astype(jnp.float32)
         moved = jnp.where(
             out_row == SPAN_LEN - 1, here[0:1], pltpu.roll(before, SPAN_LEN - 1, 0)
         )
@@ -877,18 +930,18 @@
 
 
     def drain(chunk, carry):
-        @pl.when(~is_b(chunk))
+        @pl.when(chunk < chunks_a)
         def _():
             for k in range(1, head_size):
                 lse_copy(chunk, k).wait_send()
 
         if split:
 
-            @pl.when(is_b(chunk) & middle)
+            @pl.when((chunk >= chunks_a) & middle)
             def _():
                 lse_across(chunk).wait_send()
 
-        on = ~is_b(chunk) | middle
+        on = (chunk < chunks_a) | middle
         for q in range(head_size):
             if q > 0:
 
@@ -909,10 +962,7 @@
 
 def fused(
     rows_a,
-    position,
-    order,
-    place,
-    request,
+    table,
     states,
     encodings,
     query_weight,
@@ -925,7 +975,7 @@
     slots, tokens, model = encodings.shape
     rows = states.shape[0]
     group = query_weight.shape[1]
-    entries = position.shape[0]
+    entries = table.shape[1]
     per_peer = entries // span_size
     rows_b = per_peer - rows_a
     held_b = max(rows_b, 1)
@@ -937,12 +987,11 @@
     bf16, f32 = jnp.bfloat16, jnp.float32
     dma = pltpu.SemaphoreType.DMA
     vmem = pl.BlockSpec(memory_space=pltpu.VMEM)
-    smem = pl.BlockSpec(memory_space=pltpu.SMEM)
     hbm = pl.BlockSpec(memory_space=pl.ANY)
     return pl.pallas_call(
         functools.partial(kernel, span_size, head_size, rows_a),
         out_shape=jax.ShapeDtypeStruct((blocks, SPAN_LEN, group), bf16),
-        in_specs=[smem] * 3 + [vmem] + [hbm] * 6,
+        in_specs=[vmem] + [hbm] * 6,
         out_specs=vmem,
         scratch_shapes=[
             pltpu.VMEM((slots, tokens, model), bf16),
@@ -958,16 +1007,17 @@
             pltpu.VMEM((head_size, max(span_size * rows_b, 1), tokens, 2 * group), bf16),
             pltpu.VMEM((head_size, max(span_size * rows_b, 1), tokens, 2 * group), bf16),
             pltpu.VMEM((head_size, head_size, chunk_rows, group), f32),
+            pltpu.VMEM((head_size - 2, head_size, chunk_rows, group), f32),
             pltpu.VMEM((chunks, head_size - 1, chunk_rows, group), bf16),
             pltpu.VMEM((chunks, head_size - 1, chunk_rows, group), bf16),
             pltpu.VMEM((head_size, chunks, heads, chunk_rows), f32),
-            pltpu.VMEM((2, heads, chunk_rows), f32),
-            pltpu.VMEM((2, chunk_rows, model), bf16),
+            pltpu.VMEM((chunks, heads, chunk_rows), f32),
             pltpu.VMEM((chunk_rows, score_cols), f32),
             pltpu.VMEM((chunk_rows, score_cols), bf16),
             pltpu.VMEM((blocks, SPAN_LEN, group), bf16),
-            pltpu.VMEM(request.shape, jnp.int32),
-            pltpu.SMEM(request.shape, jnp.int32),
+            pltpu.VMEM((8, 128), jnp.int32),
+            pltpu.VMEM((span_size, 8, 128), jnp.int32),
+            pltpu.SMEM((span_size, 8, 128), jnp.int32),
             dma((7,)),
             dma((span_size,)),
             dma((span_size,)),
@@ -995,10 +1045,7 @@
             flops=6 * rows * model * head_size * group, bytes_accessed=16 << 20, transcendentals=0
         ),
     )(
-        position,
-        order,
-        place,
-        request,
+        table,
         states.reshape(blocks, SPAN_LEN, model),
         encodings,
         query_weight,
@@ -1008,104 +1055,81 @@
     )
 
 
-def take(values, index):
-    numbering = jnp.arange(values.shape[0], dtype=jnp.int32)
-    return jnp.sum(jnp.where(index[:, None] == numbering[None, :], values[None, :], 0), axis=1)
-
-
-def put_at(values, index):
-    numbering = jnp.arange(values.shape[0], dtype=jnp.int32)
-    return jnp.sum(jnp.where(index[None, :] == numbering[:, None], values[None, :], 0), axis=1)
-
-
-def other_half(values):
-    return values.reshape(-1, 2)[:, ::-1].reshape(-1)
-
-
-def orbit_min(start, step, length):
-    reach = 1
-    while reach < length:
-        start = jnp.minimum(start, take(start, step))
-        reach *= 2
-        if reach < length:
-            step = take(step, step)
-    return start
-
-
-def earlier(same):
-    numbering = jnp.arange(same.shape[0], dtype=jnp.int32)
-    return jnp.sum((same & (numbering[None, :] < numbering[:, None])).astype(jnp.int32), axis=1)
-
-
-def paired(same, rank):
-    numbering = jnp.arange(rank.shape[0], dtype=jnp.int32)
-    beside = rank + 1 - 2 * (rank % 2)
-    return jnp.sum(jnp.where(same & (rank[None, :] == beside[:, None]), numbering[None, :], 0), axis=1)
-
-
-def halve(shard_ids):
-    entries = shard_ids.shape[0]
-    numbering = jnp.arange(entries, dtype=jnp.int32)
-    same = shard_ids[:, None] == shard_ids[None, :]
-    beside = paired(same, earlier(same))
-    low = orbit_min(numbering, beside + 1 - 2 * (beside % 2), entries // 2)
-    enters = low > other_half(low)
-    same = same & (enters[:, None] == enters[None, :])
-    beside = paired(same, earlier(same))
-    follow = beside + 1 - 2 * (beside % 2)
-    low = orbit_min(numbering // 2, take(follow, follow), entries // 4)
-    return (low > take(low, follow)).astype(jnp.int32)
+def plan_rows(shards, slots, per_peer, rows_a, neighbors):
+    entries = shards.shape[1]
+    shape = (entries, entries)
+    down = lax.broadcasted_iota(jnp.int32, shape, 0)
+    across = lax.broadcasted_iota(jnp.int32, shape, 1)
+    numbering = lax.broadcasted_iota(jnp.int32, (entries, 1), 0)
+    zero = jnp.zeros(shape, jnp.int32)
+
+    def total(condition, values):
+        return jnp.sum(jnp.where(condition, values, zero), axis=1, keepdims=True)
+
+    def as_row(column):
+        return jnp.sum(jnp.where(down == across, column, zero), axis=0, keepdims=True)
+
+    def put_at(column, index):
+        return jnp.sum(jnp.where(index == across, column, zero), axis=0, keepdims=True)
+
+    def take(column, index):
+        return total(index == across, as_row(column))
+
+    def earlier(same):
+        return total(same & (across < down), zero + 1)
+
+    def beside(index):
+        return index + 1 - 2 * (index % 2)
+
+    def paired(same, rank):
+        return total(same & (as_row(rank) == beside(rank)), across)
+
+    def orbit_min(start, step, length):
+        reach = 1
+        while reach < length:
+            start = jnp.minimum(start, take(start, step))
+            reach *= 2
+            if reach < length:
+                step = take(step, step)
+        return start
+
+    shard = total(down == across, shards)
+    slot = total(down == across, slots)
+    same = shard == shards
+    if rows_a < per_peer:
+        low = orbit_min(numbering, beside(paired(same, earlier(same))), entries // 2)
+        enters = (low > take(low, beside(numbering))).astype(jnp.int32)
+        kin = same & (enters == as_row(enters))
+        follow = beside(paired(kin, earlier(kin)))
+        low = orbit_min(numbering // 2, take(follow, follow), entries // 4)
+        half = (low > take(low, follow)).astype(jnp.int32)
+    else:
+        half = numbering * 0
+    alike = half == as_row(half)
+    rank = earlier(same & alike)
+    place = half * (entries // neighbors // 2) + earlier(alike) // neighbors
+    entry_place = place * neighbors + numbering % neighbors
+    request = put_at(slot, shard * per_peer + half * rows_a + rank)
+    position = put_at(shard * rows_a + rank, entry_place)
+    order = put_at(numbering // neighbors, entry_place)
+    return request, position, order, as_row(place)
 
 
 def body(
     decoder_states, encodings, neighbor_table, query_weight, key_weight, value_weight, out_weight
 ):
     peer_count = lax.axis_size("span")
-    head_size = lax.axis_size("head")
     spans, neighbors = neighbor_table.shape[:2]
-    shard_ids = neighbor_table[:, :, 0].reshape(-1)
-    slot_ids = neighbor_table[:, :, 1].reshape(-1)
-    entries = shard_ids.shape[0]
-    per_peer = entries // peer_count
+    per_peer = spans * neighbors // peer_count
     split = (
         neighbors == 2
         and per_peer % 4 == 0
-        and head_size == 4
+        and lax.axis_size("head") == 4
         and spans % (2 * CHUNK_SPANS) == 0
-        and spans >= 4 * CHUNK_SPANS
     )
-    rows_a = per_peer // 2 if split else per_peer
-    same = shard_ids[:, None] == shard_ids[None, :]
-    numbering = jnp.arange(spans, dtype=jnp.int32)
-    if split:
-        half = halve(shard_ids)
-        ranking = earlier(same & (half[:, None] == half[None, :]))
-        span_half = half.reshape(-1, 2)[:, 0]
-        span_rank = earlier(span_half[:, None] == span_half[None, :])
-        count = span_rank // CHUNK_SPANS
-        chunks = spans // CHUNK_SPANS
-        chunk = jnp.where(
-            span_half == 0,
-            jnp.maximum(2 * count - 1, 0),
-            jnp.minimum(2 * count + 2, chunks - 1),
-        )
-        place = chunk * CHUNK_SPANS + span_rank % CHUNK_SPANS
-        order = put_at(numbering, place)
-        asked_at = shard_ids * per_peer + half * rows_a + ranking
-        entry_place = (place[:, None] * 2 + jnp.arange(2, dtype=jnp.int32)[None, :]).reshape(-1)
-        position = put_at(shard_ids * rows_a + ranking, entry_place)
-    else:
-        ranking = earlier(same)
-        place = order = numbering
-        asked_at = position = shard_ids * per_peer + ranking
-    request = put_at(slot_ids, asked_at).reshape(peer_count, 1, per_peer)
-    request = jnp.pad(request, ((0, 0), (0, 7), (0, 128 - per_peer)))
     out = fused(
-        rows_a,
-        position,
-        order,
-        place,
-        request,
+        per_peer // 2 if split else per_peer,
+        neighbor_table.reshape(-1, 2).T,
         decoder_states,
         encodings,
         query_weight,

time: 163 us -> 146 us (0.90)
  Pallas kernels: 153 us -> 142 us
  other arithmetic: 4.93 us -> 0 us
  local copies, waits for them, and re-layouts: 5.48 us -> 3.7 us
    pallas_call x1, Pallas kernels: 153 us -> 142 us  [fused(): pl.pallas_call(functools.partial(kernel, span_size, head_size, rows_a), o...]
    reduce_sum x19 -> x0, other arithmetic: 4.41 us -> none  [the longest x11 1.96 us: take(): jnp.sum(jnp.where(index[:, None] == numbering[None, :], values[None, :],...]
where the time goes in v3:
time: 146 us
  Pallas kernels  142 us (97%)
  local copies, waits for them, and re-layouts  3.7 us (3%)
    pallas_call x1, Pallas kernels, fused(): pl.pallas_call(functools.partial(kernel, span_size, head_size, rows_a), o...  142 us
    unnamed x2, local copies, waits for them, and re-layouts  3.03 us

profile of v3, /device:TPU:0, one launch (start us, length us, event | category | flops | bytes accessed | tf_op | source)
XLA Modules:
  0.0 146.0 jit_solution(1411315685532314268)
XLA Ops:
  0.0 0.8 copy.9
  0.8 0.7 reshape.9
  1.4 142.3 %shard_map.73 = bf16[32,64,256]{2,1,0:T(8,128)(2,1)} custom-call(s32[2,64]{1,0:T(2,128)} %bitcast.6, bf16[32,64,1024]{2,1,0:T(8,128)(2,1)} %bitcast.7, bf16[64,32,1024]{2,1,0:T(8,128)(2,1)} %encodings_hbm.1, bf16[1024,256]{1,0:T(8,128)(2,1)} %query_hbm.1, bf16[1024,256]{1,0:T(8,128)(2,1)} %key_hbm.1, bf16[1024,256]{1,0:T(8,128)(2,1)} %value_hbm.1, ...), custom_call_target="tpu_custom_call" | custom-call | flops 12884901888 | bytes 16777216 | tf_op jit(solution)/shard_map/pallas_call | solution.py:991
  143.7 2.3 %copy.11 = bf16[2048,256]{1,0:T(8,128)(2,1)} copy(bf16[2048,256]{1,0:T(8,128)(2,1)} %bitcast.5) | data formatting | bytes 2097152
